TPU v7x, 256 devices: a whole 4x4x8 slice. The times are simulated.
256 devices in a mesh: pop: 64 (over z, y, core), tp: 4 (over x).
Axes of the slice: x: 4, y: 4, z: 8, core: 2. Of those that a mesh axis runs over, the one named last changes fastest.
Arguments:
- tokens: bfloat16 [65536, 5120], P('pop', 'tp'), may hold values from -6 to 6
- target: bfloat16 [65536, 5120], P('pop', 'tp'), may hold values from -6 to 6
- weight: bfloat16 [5120, 5120], P('pop', 'tp'), may hold values from -6 to 6
- factor_out: bfloat16 [256, 4, 5120], P('pop'), may hold values from -6 to 6
- factor_in: bfloat16 [256, 4, 5120], P('pop', None, 'tp'), may hold values from -6 to 6
Outputs:
- perturbed: bfloat16 [65536, 5120], P('pop', 'tp')
- new_weight: bfloat16 [5120, 5120], P('pop', 'tp')
All inputs are finite; a program needn't handle non-finite values.
Results may differ from a plain program's by a relative error of at most 0.012.
Values may be sent and summed in bfloat16 or wider, within the bound.
A program may use at most 128 MiB of HBM per device.

v0:
```python
import math

import jax
import jax.numpy as jnp
from jax import lax
from jax.sharding import PartitionSpec as P

noise_scale = 0.25
step_scale = 10.0


def sent_to_all(shard, axis):
    count = lax.axis_size(axis)
    return lax.all_to_all(
        jnp.broadcast_to(shard[None], (count, *shard.shape)), axis, 0, 0, tiled=True
    )


def taken_together(shard, axis):
    everything = sent_to_all(shard, axis)
    return jnp.sum(everything, axis=0)


def local(tokens, target, weight, factor_out, factor_in):
    tok_rows, shard_width = tokens.shape
    mem_local, rank, width_out = factor_out.shape
    tok_member = tok_rows // mem_local
    tp_count = lax.axis_size("tp")
    width_in = shard_width * tp_count
    out_cols = width_out // tp_count
    col_first = lax.axis_index("tp") * out_cols
    base_factor = 1.0 / math.sqrt(width_in)
    token_sets = tokens.reshape(mem_local, tok_member, shard_width)
    codes_part = jnp.einsum(
        "mkc,mrc->mkr", token_sets, factor_in, preferred_element_type=jnp.float32
    )
    codes_sum = taken_together(codes_part, "tp")
    partial_terms = (
        lax.dot_general(
            tokens,
            lax.all_gather(weight, "pop", axis=0, tiled=True),
            (((1,), (1,)), ((), ())),
            preferred_element_type=jnp.float32,
        )
        * base_factor
    )
    base_sum = lax.psum_scatter(
        partial_terms.astype(jnp.bfloat16), "tp", scatter_dimension=1, tiled=True
    ).astype(jnp.float32)
    outer_cols = lax.dynamic_slice_in_dim(factor_out, col_first, out_cols, 2).astype(jnp.float32)
    low_rank = jnp.einsum(
        "mkr,mrc->mkc", codes_sum, outer_cols, precision=lax.Precision.HIGHEST
    ) * (noise_scale / math.sqrt(rank * width_in))
    output_full = base_sum.reshape(mem_local, tok_member, out_cols) + low_rank
    wanted = target.reshape(mem_local, tok_member, out_cols).astype(jnp.float32)
    fitness_part = jnp.sum(output_full * wanted, axis=(1, 2)) / (tok_member * math.sqrt(width_out))
    fitness_grid = lax.all_gather(fitness_part[None, :], ("pop", "tp"), axis=0, tiled=True)
    fitness_all = jnp.sum(fitness_grid.reshape(-1, tp_count, mem_local), axis=1).reshape(-1)
    outer_rows = lax.all_to_all(factor_out, "pop", split_axis=2, concat_axis=0, tiled=True)
    inner_cols = lax.all_gather(factor_in, "pop", axis=0, tiled=True)
    centered = fitness_all - jnp.mean(fitness_all)
    scaled = (centered[:, None, None] * outer_rows.astype(jnp.float32)).astype(jnp.bfloat16)
    delta = jnp.einsum("imo,imc->oc", scaled, inner_cols, preferred_element_type=jnp.float32)
    members_all = fitness_all.shape[0]
    updated = (
        weight.astype(jnp.float32) + step_scale / math.sqrt(members_all * rank) * delta
    ).astype(jnp.bfloat16)
    return (output_full.reshape(tok_rows, out_cols).astype(jnp.bfloat16), updated)


def solution(mesh):
    in_specs = (
        P("pop", "tp"),
        P("pop", "tp"),
        P("pop", "tp"),
        P("pop", None, None),
        P("pop", None, "tp"),
    )
    out_specs = (P("pop", "tp"), P("pop", "tp"))
    return jax.shard_map(local, mesh=mesh, in_specs=in_specs, out_specs=out_specs, check_vma=False)
```

profile of v0, /device:TPU:1, one launch (start us, length us, event | category | flops | bytes accessed | tf_op | source)
XLA Modules:
  0.0 318.1 jit_solution(7085557132596609108)
XLA Ops:
  7.2 0.7 all-gather.4.cloned.1.call-update
  7.9 0.0 reduce-scatter.2.cloned.1.call-start
  8.0 97.6 %all-gather.4.cloned.1.call-done = bf16[5120,1280]{1,0:T(8,128)(2,1)} async-done(((bf16[80,1280]{1,0:T(8,128)(2,1)}), bf16[5120,1280]{1,0:T(8,128)(2,1)}) %all-gather.4.cloned.1.call-update) | async-done | bytes 13107216 | tf_op jit(solution)/shard_map/all_gather | solution.py:41
  105.5 20.6 %multiply_convert_fusion = bf16[1024,5120]{1,0:T(8,128)(2,1)} fusion(bf16[1024,1280]{1,0:T(8,128)(2,1)S(1)} %copy-done, bf16[5120,1280]{1,0:T(8,128)(2,1)} %all-gather.4.cloned.1.call-done), kind=kOutput, calls=%fused_computation | convolution fusion | flops 13432258560 | bytes 26214400 | tf_op jit(solution)/shard_map/dot_general | solution.py:39
  126.2 0.0 all-gather.6.cloned.1.call-start
  126.2 0.7 all-gather.6.cloned.1.call-update
  126.9 0.8 fusion.18
  127.7 0.7 broadcast_in_dim.2
  128.3 4.0 %all-to-all-start = ((f32[4,4,256,4]{2,3,1,0:T(4,128)}), f32[4,4,256,4]{2,3,1,0:T(4,128)S(1)}, u32[]{:S(2)}, u32[]{:S(2)}) async-start(f32[4,4,256,4]{2,3,1,0:T(4,128)} %broadcast_in_dim.2), calls=%async_computation.1 | async-start | bytes 131072 | tf_op jit(solution)/shard_map/all_to_all | solution.py:14
  132.3 5.2 %copy.12 = bf16[4,4,5120]{1,0,2:T(4,128)(2,1)} copy(bf16[4,4,5120]{2,1,0:T(4,128)(2,1)S(1)} %copy-done.2) | data formatting | bytes 327680 | tf_op args[3]
  137.5 11.2 %reshape.57 = bf16[64,2,640]{2,1,0:T(2,128)(2,1)} reshape(bf16[5120,4,4]{2,1,0:T(4,128)(2,1)} %bitcast.28) | data formatting | bytes 327680
  148.7 6.4 %all-to-all-start.1 = ((bf16[64,2,640]{2,1,0:T(2,128)(2,1)}), bf16[64,2,640]{2,1,0:T(2,128)(2,1)S(1)}, u32[]{:S(2)}, u32[]{:S(2)}) async-start(bf16[64,2,640]{2,1,0:T(2,128)(2,1)} %reshape.57), calls=%async_computation.2 | async-start | bytes 327680 | tf_op jit(solution)/shard_map/all_to_all | solution.py:59
  155.2 11.6 %all-to-all-done.1 = bf16[64,2,640]{2,1,0:T(2,128)(2,1)S(1)} async-done(((bf16[64,2,640]{2,1,0:T(2,128)(2,1)}), bf16[64,2,640]{2,1,0:T(2,128)(2,1)S(1)}, u32[]{:S(2)}, u32[]{:S(2)}) %all-to-all-start.1) | async-done | bytes 163872 | tf_op jit(solution)/shard_map/all_to_all | solution.py:59
  166.8 12.3 %reshape.58 = bf16[5120,4,4]{2,1,0:T(4,128)(2,1)} reshape(bf16[64,2,640]{2,1,0:T(2,128)(2,1)S(1)} %all-to-all-done.1) | data formatting | bytes 327680
  179.1 6.9 %copy.13 = f32[4,4,64,80]{3,0,2,1:T(4,128)S(1)} copy(bf16[4,4,64,80]{1,0,3,2:T(4,128)(2,1)} %bitcast.27) | data formatting | bytes 491520 | tf_op jit(solution)/shard_map/convert_element_type | solution.py:62
  186.0 37.5 %reduce-scatter.2.cloned.1.call-done = bf16[1024,1280]{1,0:T(8,128)(2,1)} async-done(((bf16[1024,5120]{1,0:T(8,128)(2,1)}), bf16[1024,1280]{1,0:T(8,128)(2,1)}) %reduce-scatter.2.cloned.1.call-update) | async-done | bytes 2621456 | tf_op jit(solution)/shard_map/reduce_scatter | solution.py:47
  223.4 7.2 %fusion = (f32[4]{0:T(128)S(1)}, bf16[4,256,1280]{2,1,0:T(8,128)(2,1)}) fusion(bf16[4,256,1280]{2,1,0:T(8,128)(2,1)} %bitcast.30, f32[4,256,4]{1,2,0:T(4,128)S(1)} %reduce_sum.36, bf16[4,4,5120]{2,1,0:T(4,128)(2,1)S(1)} %copy-done.2, s32[]{:T(128)S(6)} %select_n.3, bf16[4,256,1280]{2,1,0:T(8,128)(2,1)} %bitcast.31), kind=kOutput, calls=%fused_computation.2 | convolution fusion | flops 72089600 | bytes 7921684 | tf_op jit(solution)/shard_map/mkr,mrc->mkc/dot_general | solution.py:51
  230.6 0.1 multiply_dynamic-update-slice_fusion
  230.7 76.1 %all-reduce = f32[1024]{0:T(1024)S(1)} all-reduce(f32[1024]{0:T(1024)S(1)} %multiply_dynamic-update-slice_fusion), channel_id=2, replica_groups=mesh['pop'=64,'tp'=4] {'pop','tp'}, use_global_device_ids=true, to_apply=%add | all-reduce | flops 1024 | bytes 8192
  306.8 0.6 reduce_sum.39
  307.4 0.2 reshape.46
  307.6 0.1 reduce_sum.38
  308.3 0.1 sub.15
  308.5 3.1 fusion.12
  (15 shorter events, 0.1 us)
Async XLA Ops:
  7.2 98.4 %copy-start = (bf16[1024,1280]{1,0:T(8,128)(2,1)S(1)}, bf16[1024,1280]{1,0:T(8,128)(2,1)}, u32[]{:S(2)}) copy-start(bf16[1024,1280]{1,0:T(8,128)(2,1)} %param.5) | copy-start | bytes 7864324
  7.2 98.3 %all-gather.4.cloned.1.call-start = ((), (), s32[]{:S(2)}) async-start(), calls=%async_computation.3 | async-start | bytes 13312000 | tf_op jit(solution)/shard_map/all_gather | solution.py:41
  7.9 215.5 %reduce-scatter.2.cloned.1.call-start = ((), (), s32[]{:S(2)}) async-start(), calls=%async_computation.4 | async-start | bytes 13107200 | tf_op jit(solution)/shard_map/reduce_scatter | solution.py:47
  126.1 0.8 copy-start.3
  126.1 6.2 %copy-start.2 = (bf16[4,4,5120]{2,1,0:T(4,128)(2,1)S(1)}, bf16[4,4,5120]{2,1,0:T(4,128)(2,1)}, u32[]{:S(2)}) copy-start(bf16[4,4,5120]{2,1,0:T(4,128)(2,1)} %param.8) | copy-start | bytes 491524
  126.2 182.3 %all-gather.6.cloned.1.call-start = ((), (), s32[]{:S(2)}) async-start(), calls=%async_computation.5 | async-start | bytes 2662400 | tf_op jit(solution)/shard_map/all_gather | solution.py:60
  128.3 20.4 %all-to-all-start = ((f32[4,4,256,4]{2,3,1,0:T(4,128)}), f32[4,4,256,4]{2,3,1,0:T(4,128)S(1)}, u32[]{:S(2)}, u32[]{:S(2)}) async-start(f32[4,4,256,4]{2,3,1,0:T(4,128)} %broadcast_in_dim.2), calls=%async_computation.1 | async-start | bytes 131072 | tf_op jit(solution)/shard_map/all_to_all | solution.py:14
  148.7 18.1 %all-to-all-start.1 = ((bf16[64,2,640]{2,1,0:T(2,128)(2,1)}), bf16[64,2,640]{2,1,0:T(2,128)(2,1)S(1)}, u32[]{:S(2)}, u32[]{:S(2)}) async-start(bf16[64,2,640]{2,1,0:T(2,128)(2,1)} %reshape.57), calls=%async_computation.2 | async-start | bytes 327680 | tf_op jit(solution)/shard_map/all_to_all | solution.py:59
  186.0 122.5 %copy-start.1 = (bf16[80,1280]{1,0:T(8,128)(2,1)S(1)}, bf16[80,1280]{1,0:T(8,128)(2,1)}, u32[]{:S(2)}) copy-start(bf16[80,1280]{1,0:T(8,128)(2,1)} %param.7) | copy-start | bytes 614404
Sparse Core Ops, SparseCore 0:
  10.7 94.7 all-gather.3
  126.3 97.1 reduce-scatter.1
  226.2 77.3 all-gather.5
where the time goes:
time: 319 us; the launch traced here: 318 us
  waiting for transfers between devices  148 us (46%)
  blocking collectives  76.1 us (24%)
  local copies, waits for them, and re-layouts  36.6 us (11%)
  matrix products  31.7 us (10%)
  between operations  14.5 us (5%)
  starting transfers between devices  10.5 us (3%)
    all_gather x1, waiting for transfers between devices, local(): lax.all_gather(weight, 'pop', axis=0, tiled=True)  97.6 us
    unnamed x1, blocking collectives  76.1 us
    reduce_scatter x1, waiting for transfers between devices, local(): lax.psum_scatter(partial_terms.astype(jnp.bfloat16), 'tp', scatter_dimens...  37.5 us
    unnamed x12, local copies, waits for them, and re-layouts  28.7 us
    dot_general x1, matrix products, local(): lax.dot_general(tokens, lax.all_gather(weight, 'pop', axis=0, tiled=True)...  20.6 us
    all_to_all x1, waiting for transfers between devices, local(): lax.all_to_all(factor_out, 'pop', split_axis=2, concat_axis=0, tiled=True)  11.6 us
    dot_general x1, matrix products, local(): jnp.einsum('mkr,mrc->mkc', codes_sum, outer_cols, precision=lax.Precision...  7.16 us
    convert_element_type x1, local copies, waits for them, and re-layouts, local(): outer_rows.astype(jnp.float32)  6.9 us
  transfers between devices with their start and end apart: 5, of which 3 were waited for; matrix products, arithmetic and copies ran while one was open for 14% of the time, Pallas kernels for 0%

commit v1 on v0

v1 whole, which is shorter than its diff:
```python
import math

import jax
import jax.numpy as jnp
from jax import lax
from jax.experimental import pallas as pl
from jax.experimental.pallas import tpu as pltpu

noise_scale = 0.25
step_scale = 10.0

F32 = jnp.float32
BF16 = jnp.bfloat16
NX, NY, NZ = 4, 4, 8
NSTEP = 8


def kernel(tok, tgt, wt, fo, fin, out, neww,
           T, W, FIN, TG, WL, ACC, S32, FOS, FO2, FO3, FP, FX, FY, FZ,
           loc, tr, tl, tf, wa, wz, yu, yd, fu, fd, d2, fxs, fny, fnu, fnd, fnc,
           foy, foz, gx, gy, gz,
           s_tok, s_tf, s_wa, s_w, s_d2, s_fx, s_fny, s_fnz, s_fnc, s_foy, s_foz, s_gx, s_gy, s_gz):
    p = lax.axis_index("pop")
    x = lax.axis_index("tp")
    z = p // 8
    e = p % 8
    y = e // 2
    c = e % 2
    rows, kw = tok.shape
    mem = rows // 4
    sr = wt.shape[0]
    half = 8 * sr
    rank16 = 16
    width_in = kw * NX
    width_out = width_in

    def pop_of(zz, ee):
        return lax.rem(zz, 8) * 8 + lax.rem(ee, 8)

    def rc(src, dst, ss, rs, pop, tp):
        return pltpu.make_async_remote_copy(
            src_ref=src, dst_ref=dst, send_sem=ss, recv_sem=rs,
            device_id={"pop": pop, "tp": tp}, device_id_type=pl.DeviceIdType.MESH)

    xr = lax.rem(x + 1, 4)
    xl = lax.rem(x + 3, 4)
    zu = pop_of(z + 1, e)
    zd = pop_of(z + 7, e)
    yup = z * 8 + lax.rem(y + 1, 4) * 2 + c
    ydn = z * 8 + lax.rem(y + 3, 4) * 2 + c
    sib = z * 8 + y * 2 + (1 - c)

    l_wl = pltpu.make_async_copy(wt, WL, loc.at[0])
    l_t0 = pltpu.make_async_copy(tok, T.at[0], loc.at[1])
    l_tg = pltpu.make_async_copy(tgt, TG, loc.at[2])
    l_wl.start()
    l_t0.start()
    l_tg.start()

    bar = pltpu.get_barrier_semaphore()
    for k in range(1, 4):
        pl.semaphore_signal(bar, inc=1, device_id={"pop": p, "tp": lax.rem(x + k, 4)},
                            device_id_type=pl.DeviceIdType.MESH)
    for k in range(1, 8):
        pl.semaphore_signal(bar, inc=1, device_id={"pop": z * 8 + lax.rem(e + k, 8), "tp": x},
                            device_id_type=pl.DeviceIdType.MESH)
        pl.semaphore_signal(bar, inc=1, device_id={"pop": pop_of(z + k, e), "tp": x},
                            device_id_type=pl.DeviceIdType.MESH)
    pl.semaphore_wait(bar, 17)

    zt = z // 2
    r_own = lax.rem(z, 2)
    off = lax.rem(x - zt + 4, 4)
    slot = off + off // 2 - 2 * (off // 3)
    shard = pl.ds(pl.multiple_of(e * sr, 16), sr)
    send_a = rc(wt, W.at[slot, r_own, shard], s_wa, wa.at[slot], p, zt)
    copy_a = pltpu.make_async_copy(wt, W.at[0, r_own, shard], loc.at[3])

    @pl.when(off == 0)
    def _():
        copy_a.start()

    @pl.when(off != 0)
    def _():
        send_a.start()

    for i in range(4):
        S32[4 * i:4 * i + 4, 0:kw] = fin[i].astype(F32)
    fin16 = S32[:, 0:kw].astype(BF16)
    FP[...] = fin16
    FIN[z, y, c] = fin16
    W[0, 0, half:half + rank16] = fin16
    xslot = {1: 2, 2: 3, 3: 1}
    for k in range(1, 4):
        rc(FP, W.at[xslot[k], 0, half:half + rank16], s_fx.at[k], fxs.at[k], p, lax.rem(x + k, 4)).start()

    def chunk(m):
        return pl.ds(m * mem, mem)

    def tok_right(m):
        return rc(tok.at[chunk(m)], T.at[2, chunk(m)], s_tok.at[0, m], tr.at[m], p, xr)

    def tok_left(m):
        return rc(tok.at[chunk(m)], T.at[1, chunk(m)], s_tok.at[1, m], tl.at[m], p, xl)

    def tok_fwd(m):
        if m % 2 == 0:
            return rc(T.at[2, chunk(m)], T.at[3, chunk(m)], s_tf.at[m], tf.at[m], p, xr)
        return rc(T.at[1, chunk(m)], T.at[3, chunk(m)], s_tf.at[m], tf.at[m], p, xl)

    for m in range(4):
        tok_right(m).start()
        tok_left(m).start()

    def fin_y(k):
        return rc(FP, FIN.at[z, y, c], s_fny.at[k], fny.at[k],
                  z * 8 + lax.rem(y + k, 4) * 2 + c, x)

    def fin_y_in(k):
        return rc(FP, FIN.at[z, lax.rem(y + 4 - k, 4), c], s_fny.at[k], fny.at[k], p, x)

    for k in range(1, 4):
        fin_y(k).start()

    for i in range(4):
        S32[4 * i:4 * i + 4, :] = fo[i].astype(F32)
    grp = 8 * sr
    sel_row = lax.broadcasted_iota(jnp.int32, (grp, 1024), 0)
    sel_col = lax.broadcasted_iota(jnp.int32, (grp, 1024), 1)
    lane = lax.rem(sel_col, 128)
    want = (sel_col // 128) * sr + lane
    sel = jnp.where((sel_row == want) & (lane < sr), 1.0, 0.0).astype(BF16)
    for g in range(8):
        cut = jnp.dot(S32[:, g * grp:(g + 1) * grp].astype(BF16), sel,
                      preferred_element_type=F32).astype(BF16)
        for d in range(8):
            FOS[d, g] = cut[:, d * 128:(d + 1) * 128]
    FO2[e] = FOS[e]

    def fo_y(k):
        ee = lax.rem(e + k, 8)
        return rc(FOS.at[ee], FO2.at[e], s_foy.at[k], foy.at[k], z * 8 + ee, x)

    def fo_y_in(k):
        return rc(FOS.at[0], FO2.at[lax.rem(e + 8 - k, 8)], s_foy.at[k], foy.at[k], p, x)

    for k in range(1, 8):
        fo_y(k).start()

    def fo_z(k):
        zz = lax.rem(z + k, 8)
        return rc(FO2.at[:, zz], FO3.at[z], s_foz.at[k], foz.at[k], zz * 8 + e, x)

    def fo_z_in(k):
        return rc(FO2.at[:, 0], FO3.at[lax.rem(z + 8 - k, 8)], s_foz.at[k], foz.at[k], p, x)

    l_wl.wait()
    l_t0.wait()
    l_tg.wait()

    rz = lax.rem(z + 8 - 2 * x, 8)

    def shard_at(s, yy, cols=None):
        q = lax.rem(yy, 4) * 2 + c
        rws = pl.ds(pl.multiple_of(q * sr, 16), sr)
        ref = W.at[s // 2, s % 2, rws]
        if cols is not None:
            ref = W.at[s // 2, s % 2, rws, pl.ds(cols * (kw // 2), kw // 2)]
        return ref

    def z_in(s):
        return rc(shard_at(s, y), shard_at(s, y), s_w.at[0, s], wz.at[s], p, x)

    def z_up(s):
        return rc(shard_at(s, y), shard_at(s, y), s_w.at[0, s], wz.at[s], zu, x)

    def z_dn(s):
        return rc(shard_at(s, y), shard_at(s, y), s_w.at[1, s], wz.at[s], zd, x)

    def y_up(s):
        return rc(shard_at(s, y), shard_at(s, y), s_w.at[2, s], yu.at[s], yup, x)

    def y_up_in(s):
        return rc(shard_at(s, y + 3), shard_at(s, y + 3), s_w.at[2, s], yu.at[s], p, x)

    def y_dn(s):
        return rc(shard_at(s, y), shard_at(s, y), s_w.at[3, s], yd.at[s], ydn, x)

    def y_dn_in(s):
        return rc(shard_at(s, y + 1), shard_at(s, y + 1), s_w.at[3, s], yd.at[s], p, x)

    def f_up(s):
        return rc(shard_at(s, y + 3, 0), shard_at(s, y + 3, 0), s_w.at[4, s], fu.at[s], yup, x)

    def f_up_in(s):
        return rc(shard_at(s, y + 2, 0), shard_at(s, y + 2, 0), s_w.at[4, s], fu.at[s], p, x)

    def f_dn(s):
        return rc(shard_at(s, y + 1, 1), shard_at(s, y + 1, 1), s_w.at[5, s], fd.at[s], ydn, x)

    def f_dn_in(s):
        return rc(shard_at(s, y + 2, 1), shard_at(s, y + 2, 1), s_w.at[5, s], fd.at[s], p, x)

    def pass_on(s, k):
        return rc(shard_at(s, y + k), shard_at(s, y + k), s_d2.at[k, s], d2.at[s], sib, x)

    def sib_in(s):
        whole = W.at[s // 2, s % 2, 0:4 * sr]
        return rc(whole, whole, s_d2.at[0, s], d2.at[s], p, x)

    def up_pred(s):
        if s % 2 == 0:
            return rz <= 3
        return (rz >= 1) & (rz <= 3)

    def dn_pred(s):
        if s % 2 == 0:
            return (rz == 0) | (rz >= 6)
        return (rz <= 1) | (rz >= 6)

    def stage_a(s):
        j, r = s // 2, s % 2

        @pl.when(rz == r)
        def _():
            if j == 0:
                copy_a.wait()
            else:
                rc(shard_at(s, y), shard_at(s, y), s_wa, wa.at[j], p, x).wait_recv()

        @pl.when(rz != r)
        def _():
            z_in(s).wait_recv()

        @pl.when(up_pred(s))
        def _():
            z_up(s).start()

        @pl.when(dn_pred(s))
        def _():
            z_dn(s).start()

        y_up(s).start()
        y_dn(s).start()
        pass_on(s, 0).start()

    def stage_b(s):
        y_up_in(s).wait_recv()
        f_up(s).start()
        pass_on(s, 3).start()
        y_dn_in(s).wait_recv()
        f_dn(s).start()
        pass_on(s, 1).start()

    def stage_c(s):
        f_up_in(s).wait_recv()
        f_dn_in(s).wait_recv()
        pass_on(s, 2).start()

    def compute(s):
        j, r = s // 2, s % 2
        sib_in(s).wait_recv()
        blk = rows // 2

        def body(i, _):
            rws = pl.ds(pl.multiple_of(i * blk, blk), blk)
            prod = lax.dot_general(T[j, rws], W[j, r], (((1,), (1,)), ((), ())),
                                   preferred_element_type=F32)
            if j == 0:
                ACC[r, rws] = prod
            else:
                ACC[r, rws] += prod
            return 0

        lax.fori_loop(0, 2, body, 0)

    def fin_block(zz, lo, n):
        return FIN.at[lax.rem(zz, 8), lo:lo + n, c]

    def fin_up(h):
        lo, n = (0, 4) if h < 4 else (0, 2)
        ref = fin_block(z + 9 - h, lo, n)
        return rc(ref, ref, s_fnz.at[0, h], fnu.at[h], zu, x)

    def fin_up_in(h):
        lo, n = (0, 4) if h < 4 else (0, 2)
        ref = fin_block(z + 8 - h, lo, n)
        return rc(ref, ref, s_fnz.at[0, h], fnu.at[h], p, x)

    def fin_dn(h):
        lo, n = (0, 4) if h < 4 else (2, 2)
        ref = fin_block(z + h - 1, lo, n)
        return rc(ref, ref, s_fnz.at[1, h], fnd.at[h], zd, x)

    def fin_dn_in(h):
        lo, n = (0, 4) if h < 4 else (2, 2)
        ref = fin_block(z + h, lo, n)
        return rc(ref, ref, s_fnz.at[1, h], fnd.at[h], p, x)

    def fin_sib():
        ref = FIN.at[:, :, c]
        return rc(ref, ref, s_fnc, fnc, sib, x)

    def fin_sib_in():
        ref = FIN.at[:, :, 1 - c]
        return rc(ref, ref, s_fnc, fnc, p, x)

    base_factor = 1.0 / math.sqrt(width_in)
    low_factor = noise_scale / math.sqrt(4 * width_in)
    lanes = lax.broadcasted_iota(jnp.int32, (8, 128), 1)
    sub = lax.broadcasted_iota(jnp.int32, (8, 128), 0)

    def epilogue(r):
        cols = slice(r * half, (r + 1) * half)
        first = pl.multiple_of(x * kw + r * half, 128)
        outer = S32[:, pl.ds(first, half)].astype(BF16)
        for m in range(4):
            rws = slice(m * mem, (m + 1) * mem)
            codes = ACC[0, rws, half:half + rank16]
            col = lax.broadcasted_iota(jnp.int32, (mem, rank16), 1)
            codes = jnp.where(col // 4 == m, codes, 0.0)
            hi = codes.astype(BF16)
            lo = (codes - hi.astype(F32)).astype(BF16)
            low = jnp.dot(hi, outer, preferred_element_type=F32) + jnp.dot(
                lo, outer, preferred_element_type=F32)
            full = ACC[r, rws, 0:half] * base_factor + low * low_factor
            out[rws, cols] = full.astype(BF16)
            part = jnp.sum(full * TG[rws, cols].astype(F32)) / (mem * math.sqrt(width_out))
            FX[0] += jnp.where((sub == e) & (lanes == m), part, 0.0)

    FX[0] = jnp.zeros((8, 128), F32)

    work = {3: (0,), 4: (1,), 7: (2, 3), 8: (4, 5), 9: (6,), 10: (7,)}
    for s in range(11):
        if s < 8:
            stage_a(s)
        if 1 <= s <= 8:
            stage_b(s - 1)
        if 2 <= s <= 9:
            stage_c(s - 2)
        if s == 2:
            tr_in(tok_right, 0)
            tok_fwd(0).start()
        if s == 3:
            for k in range(1, 4):
                fin_y_in(k).wait_recv()
            for k in range(1, 4):
                rc(FP, W.at[xslot[k], 0, half:half + rank16], s_fx.at[k], fxs.at[k], p, x).wait_recv()
        if 4 <= s <= 7:
            h = s - 3
            if h > 1:
                fin_up_in(h - 1).wait_recv()
                fin_dn_in(h - 1).wait_recv()
            fin_up(h).start()
            fin_dn(h).start()
        if s == 4:
            tr_in(tok_left, 1)
            tok_fwd(1).start()
        if s == 6:
            tr_in(tok_right, 2)
            tok_fwd(2).start()
        if s == 7:
            for m in (0, 2, 3):
                tr_in(tok_left, m)
            tok_fwd(3).start()
        if s == 8:
            for k in range(1, 8):
                fo_y_in(k).wait_recv()
            for k in range(1, 8):
                fo_z(k).start()
            FO3[z] = FO2[:, z]
            for m in (1, 3):
                tr_in(tok_right, m)
        if s == 9:
            fin_up_in(4).wait_recv()
            fin_dn_in(4).wait_recv()
            fin_sib().start()
            for m in range(4):
                tok_fwd(m).wait_recv()
        for k in work.get(s, ()):
            compute(k)
        if s == 9:
            epilogue(0)
    epilogue(1)

    def g_x(k):
        return rc(FX.at[0], FX.at[k], s_gx.at[k], gx.at[k], p, lax.rem(x + k, 4))

    for k in range(1, 4):
        g_x(k).start()
    for k in range(1, 4):
        g_x(k).wait_recv()
    FY[0] = FX[0] + FX[1] + FX[2] + FX[3]

    def g_y(k):
        return rc(FY.at[0], FY.at[k], s_gy.at[k], gy.at[k], z * 8 + lax.rem(e + k, 8), x)

    for k in range(1, 8):
        g_y(k).start()
    for k in range(1, 8):
        g_y(k).wait_recv()
    plane = FY[0]
    for k in range(1, 8):
        plane = plane + FY[k]
    FP32 = plane
    FZ[z] = FP32

    def g_z(k):
        return rc(FZ.at[z], FZ.at[z], s_gz.at[k], gz.at[k], pop_of(z + k, e), x)

    def g_z_in(k):
        ref = FZ.at[lax.rem(z + 8 - k, 8)]
        return rc(ref, ref, s_gz.at[k], gz.at[k], p, x)

    for k in range(1, 8):
        g_z(k).start()
    for k in range(1, 8):
        fo_z_in(k).wait_recv()
    fin_sib_in().wait_recv()
    for k in range(1, 8):
        g_z_in(k).wait_recv()

    grid = FZ[...].reshape(64, 128)
    mean = jnp.sum(grid) / 256.0
    wide = jnp.broadcast_to(grid[:, None, :], (64, 16, 128)).reshape(1024, 128)
    rr = lax.broadcasted_iota(jnp.int32, (1024, 128), 0)
    cc = lax.broadcasted_iota(jnp.int32, (1024, 128), 1)
    mine = jnp.where(cc == lax.rem(rr, 16) // 4, wide, 0.0)
    centered = jnp.sum(mine, axis=1, keepdims=True) - mean
    scaled = (centered * FO3[...].reshape(1024, 128).astype(F32)).astype(BF16)
    delta = lax.dot_general(scaled, FIN[...].reshape(1024, kw), (((0,), (0,)), ((), ())),
                            preferred_element_type=F32)
    neww[...] = (WL[...].astype(F32) + step_scale / math.sqrt(1024.0) * delta[0:sr]).astype(BF16)

    @pl.when(off != 0)
    def _():
        send_a.wait_send()

    for k in range(1, 4):
        rc(FP, W.at[xslot[k], 0, half:half + rank16], s_fx.at[k], fxs.at[k], p, x).wait_send()
        fin_y(k).wait_send()
        g_x(k).wait_send()
    for m in range(4):
        tok_right(m).wait_send()
        tok_left(m).wait_send()
        tok_fwd(m).wait_send()
    for s in range(NSTEP):
        @pl.when(up_pred(s))
        def _():
            z_up(s).wait_send()

        @pl.when(dn_pred(s))
        def _():
            z_dn(s).wait_send()

        y_up(s).wait_send()
        y_dn(s).wait_send()
        f_up(s).wait_send()
        f_dn(s).wait_send()
        for k in range(4):
            pass_on(s, k).wait_send()
    for h in range(1, 5):
        fin_up(h).wait_send()
        fin_dn(h).wait_send()
    fin_sib().wait_send()
    for k in range(1, 8):
        fo_y(k).wait_send()
        fo_z(k).wait_send()
        g_y(k).wait_send()
        g_z(k).wait_send()


def tr_in(make, m):
    make(m).wait_recv()


def local(tokens, target, weight, factor_out, factor_in):
    rows, kw = tokens.shape
    sr = weight.shape[0]
    half = 8 * sr
    width = factor_out.shape[2]
    any_spec = pl.BlockSpec(memory_space=pl.ANY)
    vm = pl.BlockSpec(memory_space=pltpu.VMEM)
    D = pltpu.SemaphoreType.DMA
    scratch = [
        pltpu.VMEM((4, rows, kw), BF16),
        pltpu.VMEM((4, 2, half + 16, kw), BF16),
        pltpu.VMEM((8, 4, 2, 16, kw), BF16),
        pltpu.VMEM((rows, kw), BF16),
        pltpu.VMEM((sr, kw), BF16),
        pltpu.VMEM((2, rows, half + 16), F32),
        pltpu.VMEM((16, width), F32),
        pltpu.VMEM((8, 8, 16, 128), BF16),
        pltpu.VMEM((8, 8, 16, 128), BF16),
        pltpu.VMEM((8, 8, 16, 128), BF16),
        pltpu.VMEM((16, kw), BF16),
        pltpu.VMEM((4, 8, 128), F32),
        pltpu.VMEM((8, 8, 128), F32),
        pltpu.VMEM((8, 8, 128), F32),
        D((4,)), D((4,)), D((4,)), D((4,)), D((4,)), D((8,)), D((8,)), D((8,)), D((8,)), D((8,)), D((8,)),
        D((4,)), D((4,)), D((5,)), D((5,)), D(()), D((8,)), D((8,)), D((4,)), D((8,)), D((8,)),
        D((2, 4)), D((4,)), D(()), D((6, 8)), D((4, 8)), D((4,)), D((4,)), D((2, 5)), D(()),
        D((8,)), D((8,)), D((4,)), D((8,)), D((8,)),
    ]
    return pl.pallas_call(
        kernel,
        out_shape=(jax.ShapeDtypeStruct((rows, kw), BF16), jax.ShapeDtypeStruct((sr, kw), BF16)),
        in_specs=[any_spec, any_spec, any_spec, vm, vm],
        out_specs=(vm, vm),
        scratch_shapes=scratch,
        compiler_params=pltpu.CompilerParams(
            collective_id=0, has_side_effects=True, vmem_limit_bytes=62 * 1024 * 1024),
    )(tokens, target, weight, factor_out, factor_in)


def solution(mesh):
    from jax.sharding import PartitionSpec as P

    in_specs = (
        P("pop", "tp"),
        P("pop", "tp"),
        P("pop", "tp"),
        P("pop", None, None),
        P("pop", None, "tp"),
    )
    out_specs = (P("pop", "tp"), P("pop", "tp"))
    return jax.shard_map(local, mesh=mesh, in_specs=in_specs, out_specs=out_specs, check_vma=False)
```

time: 319 us -> 139 us (0.44)
  waiting for transfers between devices: 148 us -> 0 us
  Pallas kernels: 0 us -> 134 us
  blocking collectives: 76.1 us -> 0 us
  local copies, waits for them, and re-layouts: 36.6 us -> 4.12 us
  matrix products: 31.7 us -> 0 us
  between operations: 14.5 us -> 0.65 us
  starting transfers between devices: 10.5 us -> 0 us
    pallas_call x0 -> x1, Pallas kernels: none -> 134 us  [local(): pl.pallas_call(kernel, out_shape=(jax.ShapeDtypeStruct((rows, kw), BF16),...]
    all_gather x2 -> x0, waiting for transfers between devices: 97.6 us -> none  [the longest x1 97.6 us: local(): lax.all_gather(weight, 'pop', axis=0, tiled=True)]
    unnamed x1 -> x0, blocking collectives: 76.1 us -> none
    reduce_scatter x1 -> x0, waiting for transfers between devices: 37.5 us -> none  [local(): lax.psum_scatter(partial_terms.astype(jnp.bfloat16), 'tp', scatter_dimens...]
    dot_general x4 -> x0, matrix products: 31.7 us -> none  [the longest x1 20.6 us: local(): lax.dot_general(tokens, lax.all_gather(weight, 'pop', axis=0, tiled=True)...]
    unnamed x12 -> x4, local copies, waits for them, and re-layouts: 28.7 us -> 4.12 us
    all_to_all x2 -> x0, waiting for transfers between devices: 11.6 us -> none  [the longest x1 11.6 us: local(): lax.all_to_all(factor_out, 'pop', split_axis=2, concat_axis=0, tiled=True)]
    all_to_all x2 -> x0, starting transfers between devices: 10.4 us -> none  [the longest x1 6.4 us: local(): lax.all_to_all(factor_out, 'pop', split_axis=2, concat_axis=0, tiled=True)]
  transfers between devices with their start and end apart: 5 -> 0, of which waited for: 3 -> 0; matrix products, arithmetic and copies ran while one was open for 14% -> 0% of each run, Pallas kernels for 0% -> 0%
where the time goes in v1:
time: 139 us
  Pallas kernels  134 us (96%)
  local copies, waits for them, and re-layouts  4.12 us (3%)
    pallas_call x1, Pallas kernels, local(): pl.pallas_call(kernel, out_shape=(jax.ShapeDtypeStruct((rows, kw), BF16),...  134 us
    unnamed x4, local copies, waits for them, and re-layouts  4.12 us

profile of v1, /device:TPU:1, one launch (start us, length us, event | category | flops | bytes accessed | tf_op | source)
XLA Modules:
  0.0 138.8 jit_solution(18348226822813542584)
XLA Ops:
  0.6 134.0 %shard_map.68 = (bf16[1024,1280]{1,0:T(8,128)(2,1)}, bf16[80,1280]{1,0:T(8,128)(2,1)}) custom-call(bf16[1024,1280]{1,0:T(8,128)(2,1)} %tok.1, bf16[1024,1280]{1,0:T(8,128)(2,1)} %tgt.1, bf16[80,1280]{1,0:T(8,128)(2,1)} %wt.1, bf16[4,4,5120]{2,1,0:T(4,128)(2,1)} %fo.1, bf16[4,4,1280]{2,1,0:T(4,128)(2,1)} %fin.1), custom_call_target="tpu_custom_call" | custom-call | tf_op jit(solution)/shard_map/pallas_call | solution.py:505
  134.7 0.0 copy-start
  134.7 3.4 %copy.9 = bf16[1024,1280]{1,0:T(8,128)(2,1)} copy(bf16[1024,1280]{1,0:T(8,128)(2,1)} %get-tuple-element.4) | data formatting | bytes 5242880
  138.1 0.0 copy-done
  138.1 0.7 copy.10
Async XLA Ops:
  134.7 3.5 %copy-start = (bf16[80,1280]{1,0:T(8,128)(2,1)S(1)}, bf16[80,1280]{1,0:T(8,128)(2,1)}, u32[]{:S(2)}) copy-start(bf16[80,1280]{1,0:T(8,128)(2,1)} %get-tuple-element.5) | copy-start | bytes 614404

commit v2 on v1

--- a/solution.py
+++ b/solution.py
@@ -15,8 +15,8 @@
 NSTEP = 8
 
 
-def kernel(tok, tgt, wt, fo, fin, out, neww,
-           T, W, FIN, TG, WL, ACC, S32, FOS, FO2, FO3, FP, FX, FY, FZ,
+def kernel(tok, tgt, wt, fo_hbm, fin_hbm, out, neww,
+           fo, fin, T, W, FIN, TG, WL, ACC, S32, FOS, FO2, FO3, FP, FX, FY, FZ,
            loc, tr, tl, tf, wa, wz, yu, yd, fu, fd, d2, fxs, fny, fnu, fnd, fnc,
            foy, foz, gx, gy, gz,
            s_tok, s_tf, s_wa, s_w, s_d2, s_fx, s_fny, s_fnz, s_fnc, s_foy, s_foz, s_gx, s_gy, s_gz):
@@ -53,6 +53,10 @@
     l_wl = pltpu.make_async_copy(wt, WL, loc.at[0])
     l_t0 = pltpu.make_async_copy(tok, T.at[0], loc.at[1])
     l_tg = pltpu.make_async_copy(tgt, TG, loc.at[2])
+    l_fi = pltpu.make_async_copy(fin_hbm, fin, loc.at[4])
+    l_fo = pltpu.make_async_copy(fo_hbm, fo, loc.at[5])
+    l_fi.start()
+    l_fo.start()
     l_wl.start()
     l_t0.start()
     l_tg.start()
@@ -66,62 +70,14 @@
                             device_id_type=pl.DeviceIdType.MESH)
         pl.semaphore_signal(bar, inc=1, device_id={"pop": pop_of(z + k, e), "tp": x},
                             device_id_type=pl.DeviceIdType.MESH)
-    pl.semaphore_wait(bar, 17)
-
-    zt = z // 2
-    r_own = lax.rem(z, 2)
-    off = lax.rem(x - zt + 4, 4)
-    slot = off + off // 2 - 2 * (off // 3)
-    shard = pl.ds(pl.multiple_of(e * sr, 16), sr)
-    send_a = rc(wt, W.at[slot, r_own, shard], s_wa, wa.at[slot], p, zt)
-    copy_a = pltpu.make_async_copy(wt, W.at[0, r_own, shard], loc.at[3])
-
-    @pl.when(off == 0)
-    def _():
-        copy_a.start()
-
-    @pl.when(off != 0)
-    def _():
-        send_a.start()
-
+    l_fi.wait()
     for i in range(4):
         S32[4 * i:4 * i + 4, 0:kw] = fin[i].astype(F32)
     fin16 = S32[:, 0:kw].astype(BF16)
     FP[...] = fin16
     FIN[z, y, c] = fin16
     W[0, 0, half:half + rank16] = fin16
-    xslot = {1: 2, 2: 3, 3: 1}
-    for k in range(1, 4):
-        rc(FP, W.at[xslot[k], 0, half:half + rank16], s_fx.at[k], fxs.at[k], p, lax.rem(x + k, 4)).start()
-
-    def chunk(m):
-        return pl.ds(m * mem, mem)
-
-    def tok_right(m):
-        return rc(tok.at[chunk(m)], T.at[2, chunk(m)], s_tok.at[0, m], tr.at[m], p, xr)
-
-    def tok_left(m):
-        return rc(tok.at[chunk(m)], T.at[1, chunk(m)], s_tok.at[1, m], tl.at[m], p, xl)
-
-    def tok_fwd(m):
-        if m % 2 == 0:
-            return rc(T.at[2, chunk(m)], T.at[3, chunk(m)], s_tf.at[m], tf.at[m], p, xr)
-        return rc(T.at[1, chunk(m)], T.at[3, chunk(m)], s_tf.at[m], tf.at[m], p, xl)
-
-    for m in range(4):
-        tok_right(m).start()
-        tok_left(m).start()
-
-    def fin_y(k):
-        return rc(FP, FIN.at[z, y, c], s_fny.at[k], fny.at[k],
-                  z * 8 + lax.rem(y + k, 4) * 2 + c, x)
-
-    def fin_y_in(k):
-        return rc(FP, FIN.at[z, lax.rem(y + 4 - k, 4), c], s_fny.at[k], fny.at[k], p, x)
-
-    for k in range(1, 4):
-        fin_y(k).start()
-
+    l_fo.wait()
     for i in range(4):
         S32[4 * i:4 * i + 4, :] = fo[i].astype(F32)
     grp = 8 * sr
@@ -137,6 +93,56 @@
             FOS[d, g] = cut[:, d * 128:(d + 1) * 128]
     FO2[e] = FOS[e]
 
+    pl.semaphore_wait(bar, 17)
+
+    zt = z // 2
+    r_own = lax.rem(z, 2)
+    off = lax.rem(x - zt + 4, 4)
+    slot = off + off // 2 - 2 * (off // 3)
+    shard = pl.ds(pl.multiple_of(e * sr, 16), sr)
+    send_a = rc(wt, W.at[slot, r_own, shard], s_wa, wa.at[slot], p, zt)
+    copy_a = pltpu.make_async_copy(wt, W.at[0, r_own, shard], loc.at[3])
+
+    @pl.when(off == 0)
+    def _():
+        copy_a.start()
+
+    @pl.when(off != 0)
+    def _():
+        send_a.start()
+
+    xslot = {1: 2, 2: 3, 3: 1}
+    for k in range(1, 4):
+        rc(FP, W.at[xslot[k], 0, half:half + rank16], s_fx.at[k], fxs.at[k], p, lax.rem(x + k, 4)).start()
+
+    def chunk(m):
+        return pl.ds(m * mem, mem)
+
+    def tok_right(m):
+        return rc(tok.at[chunk(m)], T.at[2, chunk(m)], s_tok.at[0, m], tr.at[m], p, xr)
+
+    def tok_left(m):
+        return rc(tok.at[chunk(m)], T.at[1, chunk(m)], s_tok.at[1, m], tl.at[m], p, xl)
+
+    def tok_fwd(m):
+        if m % 2 == 0:
+            return rc(T.at[2, chunk(m)], T.at[3, chunk(m)], s_tf.at[m], tf.at[m], p, xr)
+        return rc(T.at[1, chunk(m)], T.at[3, chunk(m)], s_tf.at[m], tf.at[m], p, xl)
+
+    for m in (0, 2, 1, 3):
+        tok_right(m).start()
+        tok_left(3 - m).start()
+
+    def fin_y(k):
+        return rc(FP, FIN.at[z, y, c], s_fny.at[k], fny.at[k],
+                  z * 8 + lax.rem(y + k, 4) * 2 + c, x)
+
+    def fin_y_in(k):
+        return rc(FP, FIN.at[z, lax.rem(y + 4 - k, 4), c], s_fny.at[k], fny.at[k], p, x)
+
+    for k in range(1, 4):
+        fin_y(k).start()
+
     def fo_y(k):
         ee = lax.rem(e + k, 8)
         return rc(FOS.at[ee], FO2.at[e], s_foy.at[k], foy.at[k], z * 8 + ee, x)
@@ -257,19 +263,21 @@
         f_dn_in(s).wait_recv()
         pass_on(s, 2).start()
 
+    def product(s, rws):
+        j, r = s // 2, s % 2
+        prod = lax.dot_general(T[j, rws], W[j, r], (((1,), (1,)), ((), ())),
+                               preferred_element_type=F32)
+        if j == 0:
+            ACC[r, rws] = prod
+        else:
+            ACC[r, rws] += prod
+
     def compute(s):
-        j, r = s // 2, s % 2
         sib_in(s).wait_recv()
         blk = rows // 2
 
         def body(i, _):
-            rws = pl.ds(pl.multiple_of(i * blk, blk), blk)
-            prod = lax.dot_general(T[j, rws], W[j, r], (((1,), (1,)), ((), ())),
-                                   preferred_element_type=F32)
-            if j == 0:
-                ACC[r, rws] = prod
-            else:
-                ACC[r, rws] += prod
+            product(s, pl.ds(pl.multiple_of(i * blk, blk), blk))
             return 0
 
         lax.fori_loop(0, 2, body, 0)
@@ -310,17 +318,16 @@
     lanes = lax.broadcasted_iota(jnp.int32, (8, 128), 1)
     sub = lax.broadcasted_iota(jnp.int32, (8, 128), 0)
 
-    def epilogue(r):
-        cols = slice(r * half, (r + 1) * half)
-        first = pl.multiple_of(x * kw + r * half, 128)
-        outer = S32[:, pl.ds(first, half)].astype(BF16)
-        for m in range(4):
-            rws = slice(m * mem, (m + 1) * mem)
-            codes = ACC[0, rws, half:half + rank16]
-            col = lax.broadcasted_iota(jnp.int32, (mem, rank16), 1)
-            codes = jnp.where(col // 4 == m, codes, 0.0)
-            hi = codes.astype(BF16)
-            lo = (codes - hi.astype(F32)).astype(BF16)
+    def epilogue(m):
+        rws = slice(m * mem, (m + 1) * mem)
+        codes = ACC[0, rws, half:half + rank16]
+        col = lax.broadcasted_iota(jnp.int32, (mem, rank16), 1)
+        codes = jnp.where(col // 4 == m, codes, 0.0)
+        hi = codes.astype(BF16)
+        lo = (codes - hi.astype(F32)).astype(BF16)
+        for r in range(2):
+            cols = slice(r * half, (r + 1) * half)
+            outer = S32[:, pl.ds(pl.multiple_of(x * kw + r * half, 128), half)].astype(BF16)
             low = jnp.dot(hi, outer, preferred_element_type=F32) + jnp.dot(
                 lo, outer, preferred_element_type=F32)
             full = ACC[r, rws, 0:half] * base_factor + low * low_factor
@@ -329,59 +336,101 @@
             FX[0] += jnp.where((sub == e) & (lanes == m), part, 0.0)
 
     FX[0] = jnp.zeros((8, 128), F32)
-
-    work = {3: (0,), 4: (1,), 7: (2, 3), 8: (4, 5), 9: (6,), 10: (7,)}
-    for s in range(11):
-        if s < 8:
-            stage_a(s)
-        if 1 <= s <= 8:
-            stage_b(s - 1)
-        if 2 <= s <= 9:
-            stage_c(s - 2)
-        if s == 2:
-            tr_in(tok_right, 0)
-            tok_fwd(0).start()
-        if s == 3:
+    far = (rz >= 3) & (rz <= 6)
+
+    def forward(ms):
+        for m in ms:
+            (tok_left if m % 2 else tok_right)(m).wait_recv()
+            tok_fwd(m).start()
+
+    def fwd_far(*ms):
+        @pl.when(far)
+        def _():
+            forward(ms)
+
+    def fwd_near(*ms):
+        @pl.when(jnp.logical_not(far))
+        def _():
+            forward(ms)
+
+    def fin_hop(h):
+        if h == 1:
             for k in range(1, 4):
                 fin_y_in(k).wait_recv()
-            for k in range(1, 4):
-                rc(FP, W.at[xslot[k], 0, half:half + rank16], s_fx.at[k], fxs.at[k], p, x).wait_recv()
-        if 4 <= s <= 7:
-            h = s - 3
-            if h > 1:
-                fin_up_in(h - 1).wait_recv()
-                fin_dn_in(h - 1).wait_recv()
-            fin_up(h).start()
-            fin_dn(h).start()
-        if s == 4:
-            tr_in(tok_left, 1)
-            tok_fwd(1).start()
-        if s == 6:
-            tr_in(tok_right, 2)
-            tok_fwd(2).start()
-        if s == 7:
-            for m in (0, 2, 3):
-                tr_in(tok_left, m)
-            tok_fwd(3).start()
-        if s == 8:
-            for k in range(1, 8):
-                fo_y_in(k).wait_recv()
-            for k in range(1, 8):
-                fo_z(k).start()
-            FO3[z] = FO2[:, z]
-            for m in (1, 3):
-                tr_in(tok_right, m)
-        if s == 9:
-            fin_up_in(4).wait_recv()
-            fin_dn_in(4).wait_recv()
-            fin_sib().start()
-            for m in range(4):
-                tok_fwd(m).wait_recv()
-        for k in work.get(s, ()):
-            compute(k)
-        if s == 9:
-            epilogue(0)
-    epilogue(1)
+        else:
+            fin_up_in(h - 1).wait_recv()
+            fin_dn_in(h - 1).wait_recv()
+        fin_up(h).start()
+        fin_dn(h).start()
+
+    def tokens_in():
+        for k in range(1, 4):
+            rc(FP, W.at[xslot[k], 0, half:half + rank16], s_fx.at[k], fxs.at[k], p, x).wait_recv()
+        for m in (0, 2):
+            tok_left(m).wait_recv()
+
+    def fo_hop():
+        for k in range(1, 8):
+            fo_y_in(k).wait_recv()
+        for k in range(1, 8):
+            fo_z(k).start()
+        FO3[z] = FO2[:, z]
+
+    A, B, C = stage_a, stage_b, stage_c
+    A(0)
+    A(1)
+    B(0)
+    A(2)
+    A(3)
+    fin_hop(1)
+    B(1)
+    fwd_far(0, 1)
+    C(0)
+    A(4)
+    B(2)
+    A(5)
+    C(1)
+    fwd_far(2, 3)
+    fwd_near(0, 1)
+    A(6)
+    B(3)
+    fin_hop(2)
+    C(2)
+    A(7)
+    compute(0)
+    B(4)
+    C(3)
+    compute(1)
+    fin_hop(3)
+    B(5)
+    C(4)
+    fwd_near(2, 3)
+    B(6)
+    fin_hop(4)
+    C(5)
+    tokens_in()
+    compute(2)
+    B(7)
+    compute(3)
+    C(6)
+    fo_hop()
+    for m in (1, 3):
+        tok_right(m).wait_recv()
+    compute(4)
+    C(7)
+    compute(5)
+    fin_up_in(4).wait_recv()
+    fin_dn_in(4).wait_recv()
+    fin_sib().start()
+    sib_in(6).wait_recv()
+    sib_in(7).wait_recv()
+    for pair in ((0, 1), (2, 3)):
+        for m in pair:
+            tok_fwd(m).wait_recv()
+        for m in pair:
+            for k in (6, 7):
+                product(k, pl.ds(m * mem, mem))
+            epilogue(m)
 
     def g_x(k):
         return rc(FX.at[0], FX.at[k], s_gx.at[k], gx.at[k], p, lax.rem(x + k, 4))
@@ -470,19 +519,17 @@
         g_z(k).wait_send()
 
 
-def tr_in(make, m):
-    make(m).wait_recv()
-
-
 def local(tokens, target, weight, factor_out, factor_in):
     rows, kw = tokens.shape
     sr = weight.shape[0]
     half = 8 * sr
     width = factor_out.shape[2]
-    any_spec = pl.BlockSpec(memory_space=pl.ANY)
+    any_spec = pl.BlockSpec(memory_space=pltpu.HBM)
     vm = pl.BlockSpec(memory_space=pltpu.VMEM)
     D = pltpu.SemaphoreType.DMA
     scratch = [
+        pltpu.VMEM(factor_out.shape, BF16),
+        pltpu.VMEM(factor_in.shape, BF16),
         pltpu.VMEM((4, rows, kw), BF16),
         pltpu.VMEM((4, 2, half + 16, kw), BF16),
         pltpu.VMEM((8, 4, 2, 16, kw), BF16),
@@ -497,19 +544,19 @@
         pltpu.VMEM((4, 8, 128), F32),
         pltpu.VMEM((8, 8, 128), F32),
         pltpu.VMEM((8, 8, 128), F32),
-        D((4,)), D((4,)), D((4,)), D((4,)), D((4,)), D((8,)), D((8,)), D((8,)), D((8,)), D((8,)), D((8,)),
+        D((6,)), D((4,)), D((4,)), D((4,)), D((4,)), D((8,)), D((8,)), D((8,)), D((8,)), D((8,)), D((8,)),
         D((4,)), D((4,)), D((5,)), D((5,)), D(()), D((8,)), D((8,)), D((4,)), D((8,)), D((8,)),
         D((2, 4)), D((4,)), D(()), D((6, 8)), D((4, 8)), D((4,)), D((4,)), D((2, 5)), D(()),
         D((8,)), D((8,)), D((4,)), D((8,)), D((8,)),
     ]
     return pl.pallas_call(
         kernel,
-        out_shape=(jax.ShapeDtypeStruct((rows, kw), BF16), jax.ShapeDtypeStruct((sr, kw), BF16)),
-        in_specs=[any_spec, any_spec, any_spec, vm, vm],
+        out_shape=(pltpu.VMEM((rows, kw), BF16), pltpu.VMEM((sr, kw), BF16)),
+        in_specs=[any_spec] * 5,
         out_specs=(vm, vm),
         scratch_shapes=scratch,
         compiler_params=pltpu.CompilerParams(
-            collective_id=0, has_side_effects=True, vmem_limit_bytes=62 * 1024 * 1024),
+            collective_id=0, has_side_effects=True, vmem_limit_bytes=56 * 1024 * 1024),
     )(tokens, target, weight, factor_out, factor_in)
 
 

time: 139 us -> 128 us (0.921)
  Pallas kernels: 134 us -> 125 us
  local copies, waits for them, and re-layouts: 4.12 us -> 2.17 us
    pallas_call x1, Pallas kernels: 134 us -> 125 us  [local(): pl.pallas_call(kernel, out_shape=(pltpu.VMEM((rows, kw), BF16), pltpu.VME...]
    unnamed x4 -> x2, local copies, waits for them, and re-layouts: 4.12 us -> 2.17 us
where the time goes in v2:
time: 128 us
  Pallas kernels  125 us (98%)
  local copies, waits for them, and re-layouts  2.17 us (2%)
    pallas_call x1, Pallas kernels, local(): pl.pallas_call(kernel, out_shape=(pltpu.VMEM((rows, kw), BF16), pltpu.VME...  125 us

profile of v2, /device:TPU:1, one launch (start us, length us, event | category | flops | bytes accessed | tf_op | source)
XLA Modules:
  0.0 127.8 jit_solution(9288472602222673621)
XLA Ops:
  0.6 125.0 %shard_map.68 = (bf16[1024,1280]{1,0:T(8,128)(2,1)S(1)}, bf16[80,1280]{1,0:T(8,128)(2,1)S(1)}) custom-call(bf16[1024,1280]{1,0:T(8,128)(2,1)} %tok.1, bf16[1024,1280]{1,0:T(8,128)(2,1)} %tgt.1, bf16[80,1280]{1,0:T(8,128)(2,1)} %wt.1, bf16[4,4,5120]{2,1,0:T(4,128)(2,1)} %fo_hbm.1, bf16[4,4,1280]{2,1,0:T(4,128)(2,1)} %fin_hbm.1), custom_call_target="tpu_custom_call" | custom-call | tf_op jit(solution)/shard_map/pallas_call | solution.py:552
  125.6 1.5 %copy.9 = bf16[1024,1280]{1,0:T(8,128)(2,1)} copy(bf16[1024,1280]{1,0:T(8,128)(2,1)S(1)} %get-tuple-element.2) | data formatting | bytes 5242880
  127.1 0.7 copy.10

commit v3 on v2

v3 whole, which is shorter than its diff:
```python
import math

import jax
import jax.numpy as jnp
from jax import lax
from jax.experimental import pallas as pl
from jax.experimental.pallas import tpu as pltpu

noise_scale = 0.25
step_scale = 10.0

F32 = jnp.float32
BF16 = jnp.bfloat16
NX, NY, NZ = 4, 4, 8
NSTEP = 8


def kernel(tok, tgt, wt, fo_hbm, fin_hbm, out, neww,
           fo, fin, T, W, FIN, TG, WL, ACC, S32, FOS, FO2, FO3, FP, FX, FZ,
           loc, tr, tl, tf, wa, wz, yin, ff, d2, fxs, fny, fnu, fnd, fnc,
           foy, foz, gx, gz,
           s_tok, s_tf, s_wa, s_z, s_y, s_f, s_d2, s_fx, s_fny, s_fnz, s_fnc, s_foy, s_foz, s_gx, s_gz):
    p = lax.axis_index("pop")
    x = lax.axis_index("tp")
    z = p // 8
    e = p % 8
    y = e // 2
    c = e % 2
    rows, kw = tok.shape
    mem = rows // 4
    sr = wt.shape[0]
    half = 8 * sr
    rank16 = 16
    width_in = kw * NX
    width_out = width_in

    def pop_of(zz, ee):
        return lax.rem(zz, 8) * 8 + lax.rem(ee, 8)

    def rc(src, dst, ss, rs, pop, tp):
        return pltpu.make_async_remote_copy(
            src_ref=src, dst_ref=dst, send_sem=ss, recv_sem=rs,
            device_id={"pop": pop, "tp": tp}, device_id_type=pl.DeviceIdType.MESH)

    xr = lax.rem(x + 1, 4)
    xl = lax.rem(x + 3, 4)
    zu = pop_of(z + 1, e)
    zd = pop_of(z + 7, e)
    yup = z * 8 + lax.rem(y + 1, 4) * 2 + c
    ydn = z * 8 + lax.rem(y + 3, 4) * 2 + c
    sib = z * 8 + y * 2 + (1 - c)

    l_wl = pltpu.make_async_copy(wt, WL, loc.at[0])
    l_t0 = pltpu.make_async_copy(tok, T.at[0], loc.at[1])
    l_tg = pltpu.make_async_copy(tgt, TG, loc.at[2])
    l_fi = pltpu.make_async_copy(fin_hbm, fin, loc.at[4])
    l_fo = pltpu.make_async_copy(fo_hbm, fo, loc.at[5])
    l_fi.start()
    l_fo.start()
    l_wl.start()
    l_t0.start()
    l_tg.start()

    bar = pltpu.get_barrier_semaphore()
    def xy_peer(k):
        return z * 8 + lax.rem(y + k // 4, 4) * 2 + c, lax.rem(x + k % 4, 4)

    def zc_peer(k):
        return lax.rem(z + k % 8, 8) * 8 + y * 2 + lax.rem(c + k // 8, 2)

    partners = [xy_peer(k) for k in range(1, 16)] + [(zc_peer(k), x) for k in range(1, 16)]
    partners += [(z * 8 + lax.rem(y + k, 4) * 2 + 1 - c, x) for k in range(1, 4)]
    for pop, tp in partners:
        pl.semaphore_signal(bar, inc=1, device_id={"pop": pop, "tp": tp},
                            device_id_type=pl.DeviceIdType.MESH)
    l_fi.wait()
    for i in range(4):
        S32[4 * i:4 * i + 4, 0:kw] = fin[i].astype(F32)
    fin16 = S32[:, 0:kw].astype(BF16)
    FP[...] = fin16
    FIN[z, y, c] = fin16
    W[0, 0, half:half + rank16] = fin16
    pl.semaphore_wait(bar, 33)

    zt = z // 2
    r_own = lax.rem(z, 2)
    off = lax.rem(x - zt + 4, 4)
    slot = off + off // 2 - 2 * (off // 3)
    shard = pl.ds(pl.multiple_of(e * sr, 16), sr)
    send_a = rc(wt, W.at[slot, r_own, shard], s_wa, wa.at[slot], p, zt)
    copy_a = pltpu.make_async_copy(wt, W.at[0, r_own, shard], loc.at[3])

    @pl.when(off == 0)
    def _():
        copy_a.start()

    @pl.when(off != 0)
    def _():
        send_a.start()

    xslot = {1: 2, 2: 3, 3: 1}
    for k in range(1, 4):
        rc(FP, W.at[xslot[k], 0, half:half + rank16], s_fx, fxs.at[k], p, lax.rem(x + k, 4)).start()

    def chunk(m):
        return pl.ds(m * mem, mem)

    def tok_right(m):
        return rc(tok.at[chunk(m)], T.at[2, chunk(m)], s_tok.at[0, m], tr.at[m], p, xr)

    def tok_left(m):
        return rc(tok.at[chunk(m)], T.at[1, chunk(m)], s_tok.at[1, m], tl.at[m], p, xl)

    small = mem // 2
    pieces = ((0, 0, mem), (3, 3 * mem, mem), (1, mem, small), (2, 2 * mem + small, small),
              (1, mem + small, small), (2, 2 * mem, small))

    def tok_fwd(i):
        m, first, n = pieces[i]
        rws = pl.ds(first, n)
        side, to = (1, xl) if m >= 2 else (2, xr)
        return rc(T.at[side, rws], T.at[3, rws], s_tf.at[i], tf.at[i], p, to)

    for m in range(4):
        tok_right(m).start()
        tok_left(3 - m).start()

    def fin_y(k):
        return rc(FP, FIN.at[z, y, c], s_fny, fny.at[k],
                  z * 8 + lax.rem(y + k, 4) * 2 + c, x)

    def fin_y_in(k):
        return rc(FP, FIN.at[z, lax.rem(y + 4 - k, 4), c], s_fny, fny.at[k], p, x)

    for k in range(1, 4):
        fin_y(k).start()

    def fo_y(k):
        ee = lax.rem(e + k, 8)
        return rc(FOS.at[ee], FO2.at[e], s_foy, foy.at[k], z * 8 + ee, x)

    def fo_y_in(k):
        return rc(FOS.at[0], FO2.at[lax.rem(e + 8 - k, 8)], s_foy, foy.at[k], p, x)

    def fo_cut():
        l_fo.wait()
        for i in range(4):
            S32[4 * i:4 * i + 4, :] = fo[i].astype(F32)
        grp = 8 * sr
        sel_row = lax.broadcasted_iota(jnp.int32, (grp, 1024), 0)
        sel_col = lax.broadcasted_iota(jnp.int32, (grp, 1024), 1)
        lane = lax.rem(sel_col, 128)
        want = (sel_col // 128) * sr + lane
        sel = jnp.where((sel_row == want) & (lane < sr), 1.0, 0.0).astype(BF16)
        for g in range(8):
            cut = jnp.dot(S32[:, g * grp:(g + 1) * grp].astype(BF16), sel,
                          preferred_element_type=F32).astype(BF16)
            for d in range(8):
                FOS[d, g] = cut[:, d * 128:(d + 1) * 128]
        FO2[e] = FOS[e]
        for k in range(1, 8):
            fo_y(k).start()

    def fo_z(k):
        zz = lax.rem(z + k, 8)
        return rc(FO2.at[:, zz], FO3.at[z], s_foz, foz.at[k], zz * 8 + e, x)

    def fo_z_in(k):
        return rc(FO2.at[:, 0], FO3.at[lax.rem(z + 8 - k, 8)], s_foz, foz.at[k], p, x)

    l_wl.wait()
    l_t0.wait()
    l_tg.wait()

    rz = lax.rem(z + 8 - 2 * x, 8)

    def shard_at(s, yy, h=None):
        q = lax.rem(yy, 4) * 2 + c
        rws = pl.ds(pl.multiple_of(q * sr, 16), sr)
        if h is None:
            return W.at[s // 2, s % 2, rws]
        return W.at[s // 2, s % 2, rws, pl.ds(h * (kw // 2), kw // 2)]

    def piece(s, yy, h, ss, rs, pop):
        return rc(shard_at(s, yy, h), shard_at(s, yy, h), ss, rs, pop, x)

    def z_send(s, h, d):
        return piece(s, y, h, s_z.at[d, 2 * s + h], wz.at[2 * s + h], (zu, zd)[d])

    def z_in(s, h):
        return piece(s, y, h, s_z.at[0, 2 * s + h], wz.at[2 * s + h], p)

    def y_send(s, h, d):
        return piece(s, y, h, s_y.at[d], yin.at[d, 2 * s + h], (yup, ydn)[d])

    def y_in(s, h, d):
        return piece(s, y + (3, 1)[d], h, s_y.at[d], yin.at[d, 2 * s + h], p)

    def f_send(s, d):
        return piece(s, y + (3, 1)[d], d, s_f.at[d], ff.at[d, s], (yup, ydn)[d])

    def f_in(s, d):
        return piece(s, y + 2, d, s_f.at[d], ff.at[d, s], p)

    def pass_on(s, k):
        return rc(shard_at(s, y + k), shard_at(s, y + k), s_d2.at[s], d2.at[s], sib, x)

    def sib_in(s):
        whole = W.at[s // 2, s % 2, 0:4 * sr]
        return rc(whole, whole, s_d2.at[s], d2.at[s], p, x)

    def z_pred(s, d):
        if d == 0:
            return rz <= 3 if s % 2 == 0 else (rz >= 1) & (rz <= 3)
        return (rz == 0) | (rz >= 6) if s % 2 == 0 else (rz <= 1) | (rz >= 6)

    def stage_a(s, h):
        j, r = s // 2, s % 2

        if h == 0:
            @pl.when(rz == r)
            def _():
                if j == 0:
                    copy_a.wait()
                else:
                    rc(shard_at(s, y), shard_at(s, y), s_wa, wa.at[j], p, x).wait_recv()

        @pl.when(rz != r)
        def _():
            z_in(s, h).wait_recv()

        for d in range(2):
            @pl.when(z_pred(s, d))
            def _():
                z_send(s, h, d).start()

        for d in range(2):
            y_send(s, h, d).start()
        if h == 1:
            pass_on(s, 0).start()

    def stage_b(s, h):
        for d in range(2):
            y_in(s, h, d).wait_recv()
            if d == h:
                f_send(s, d).start()
        if h == 1:
            pass_on(s, 3).start()
            pass_on(s, 1).start()

    def stage_c(s):
        for d in range(2):
            f_in(s, d).wait_recv()
        pass_on(s, 2).start()

    def product(s, rws):
        j, r = s // 2, s % 2
        prod = lax.dot_general(T[j, rws], W[j, r], (((1,), (1,)), ((), ())),
                               preferred_element_type=F32)
        if j == 0:
            ACC[r, rws] = prod
        else:
            ACC[r, rws] += prod

    def compute(s):
        sib_in(s).wait_recv()
        blk = rows // 2

        def body(i, _):
            product(s, pl.ds(pl.multiple_of(i * blk, blk), blk))
            return 0

        lax.fori_loop(0, 2, body, 0)

    def fin_block(zz, lo, n):
        return FIN.at[lax.rem(zz, 8), lo:lo + n, c]

    def fin_up(h):
        lo, n = (0, 4) if h < 4 else (0, 2)
        ref = fin_block(z + 9 - h, lo, n)
        return rc(ref, ref, s_fnz.at[0, h], fnu.at[h], zu, x)

    def fin_up_in(h):
        lo, n = (0, 4) if h < 4 else (0, 2)
        ref = fin_block(z + 8 - h, lo, n)
        return rc(ref, ref, s_fnz.at[0, h], fnu.at[h], p, x)

    def fin_dn(h):
        lo, n = (0, 4) if h < 4 else (2, 2)
        ref = fin_block(z + h - 1, lo, n)
        return rc(ref, ref, s_fnz.at[1, h], fnd.at[h], zd, x)

    def fin_dn_in(h):
        lo, n = (0, 4) if h < 4 else (2, 2)
        ref = fin_block(z + h, lo, n)
        return rc(ref, ref, s_fnz.at[1, h], fnd.at[h], p, x)

    def fin_sib():
        ref = FIN.at[:, :, c]
        return rc(ref, ref, s_fnc, fnc, sib, x)

    def fin_sib_in():
        ref = FIN.at[:, :, 1 - c]
        return rc(ref, ref, s_fnc, fnc, p, x)

    base_factor = 1.0 / math.sqrt(width_in)
    low_factor = noise_scale / math.sqrt(4 * width_in)
    lanes = lax.broadcasted_iota(jnp.int32, (8, 128), 1)
    sub = lax.broadcasted_iota(jnp.int32, (8, 128), 0)

    def epilogue(m, first, n):
        rws = slice(first, first + n)
        codes = ACC[0, rws, half:half + rank16]
        col = lax.broadcasted_iota(jnp.int32, (n, rank16), 1)
        codes = jnp.where(col // 4 == m, codes, 0.0)
        hi = codes.astype(BF16)
        lo = (codes - hi.astype(F32)).astype(BF16)
        for r in range(2):
            cols = slice(r * half, (r + 1) * half)
            outer = S32[:, pl.ds(pl.multiple_of(x * kw + r * half, 128), half)].astype(BF16)
            low = jnp.dot(hi, outer, preferred_element_type=F32) + jnp.dot(
                lo, outer, preferred_element_type=F32)
            full = ACC[r, rws, 0:half] * base_factor + low * low_factor
            out[rws, cols] = full.astype(BF16)
            part = jnp.sum(full * TG[rws, cols].astype(F32)) / (mem * math.sqrt(width_out))
            FX[0] += jnp.where((sub == e) & (lanes == m), part, 0.0)

    FX[0] = jnp.zeros((8, 128), F32)

    zone = (rz <= 1, (rz == 2) | (rz == 7), (rz >= 3) & (rz <= 6))

    def fwd(which, pair):
        @pl.when(zone[which])
        def _():
            for m in ((0, 3), (1, 2))[pair]:
                (tok_left if m >= 2 else tok_right)(m).wait_recv()
            for i in ((0, 1), (2, 3, 4, 5))[pair]:
                tok_fwd(i).start()

    def fin_hop(h):
        if h == 1:
            for k in range(1, 4):
                fin_y_in(k).wait_recv()
        else:
            fin_up_in(h - 1).wait_recv()
            fin_dn_in(h - 1).wait_recv()
        fin_up(h).start()
        fin_dn(h).start()

    def tokens_in():
        for k in range(1, 4):
            rc(FP, W.at[xslot[k], 0, half:half + rank16], s_fx, fxs.at[k], p, x).wait_recv()
        for m in (0, 1):
            tok_left(m).wait_recv()

    def fo_hop():
        for k in range(1, 8):
            fo_y_in(k).wait_recv()
        for k in range(1, 8):
            fo_z(k).start()
        FO3[z] = FO2[:, z]

    A, B, C = stage_a, stage_b, stage_c
    A(0, 0)
    A(0, 1)
    fo_cut()
    A(1, 0)
    B(0, 0)
    A(1, 1)
    B(0, 1)
    fwd(2, 0)
    A(2, 0)
    fin_hop(1)
    B(1, 0)
    A(2, 1)
    C(0)
    B(1, 1)
    A(3, 0)
    fwd(1, 0)
    A(3, 1)
    B(2, 0)
    C(1)
    A(4, 0)
    B(2, 1)
    fwd(2, 1)
    A(4, 1)
    B(3, 0)
    fwd(0, 0)
    A(5, 0)
    C(2)
    fin_hop(2)
    B(3, 1)
    A(5, 1)
    A(6, 0)
    B(4, 0)
    C(3)
    fwd(1, 1)
    A(6, 1)
    compute(0)
    B(4, 1)
    A(7, 0)
    compute(1)
    B(5, 0)
    A(7, 1)
    C(4)
    fwd(0, 1)
    B(5, 1)
    fin_hop(3)
    B(6, 0)
    C(5)
    B(6, 1)
    tokens_in()
    compute(2)
    B(7, 0)
    C(6)
    compute(3)
    B(7, 1)
    for m in (2, 3):
        tok_right(m).wait_recv()
    compute(4)
    compute(5)
    fin_hop(4)
    C(7)
    fo_hop()
    sib_in(6).wait_recv()
    sib_in(7).wait_recv()
    for pair in ((0, 1), (2, 3), (4, 5)):
        for i in pair:
            tok_fwd(i).wait_recv()
        if pair[0] == 4:
            for k in (6, 7):
                product(k, pl.ds(mem + small, mem))
        for i in pair:
            m, first, n = pieces[i]
            if pair[0] < 4:
                for k in (6, 7):
                    product(k, pl.ds(first, n))
            epilogue(m, first, n)
        if pair[0] == 0:
            fin_up_in(4).wait_recv()
            fin_dn_in(4).wait_recv()
            fin_sib().start()

    def g_x(k):
        pop, tp = xy_peer(k)
        return rc(FX.at[0], FX.at[k], s_gx, gx.at[k], pop, tp)

    for k in range(1, 16):
        g_x(k).start()
    for k in range(1, 16):
        g_x(k).wait_recv()
    plane = FX[0]
    for k in range(1, 16):
        plane = plane + FX[k]
    FZ[z * 2 + c] = plane

    def g_z(k):
        ref = FZ.at[z * 2 + c]
        return rc(ref, ref, s_gz, gz.at[k], zc_peer(k), x)

    def g_z_in(k):
        ref = FZ.at[lax.rem(z + 8 - k % 8, 8) * 2 + lax.rem(c + k // 8, 2)]
        return rc(ref, ref, s_gz, gz.at[k], p, x)

    for k in range(1, 16):
        g_z(k).start()
    def left(ref, sem):
        rc(ref, ref, sem, fnc, p, x).wait_send()

    @pl.when(off != 0)
    def _():
        send_a.wait_send()

    left(FIN.at[0, 0:3, 0], s_fx)
    left(FIN.at[0, 0:3, 0], s_fny)
    for m in range(4):
        tok_right(m).wait_send()
        tok_left(m).wait_send()
    for i in range(6):
        tok_fwd(i).wait_send()
    for s in range(NSTEP):
        for d in range(2):
            for h in range(2):
                @pl.when(z_pred(s, d))
                def _():
                    z_send(s, h, d).wait_send()
        left(W.at[0, 0, 0:4 * sr], s_d2.at[s])
    for d in range(2):
        left(W.at[0, 0, 0:8 * sr], s_y.at[d])
        left(W.at[0, 0, 0:4 * sr], s_f.at[d])
    for h in range(1, 5):
        fin_up(h).wait_send()
        fin_dn(h).wait_send()
    fin_sib().wait_send()
    left(FOS.at[0:7], s_foy)
    left(FO3.at[0:7], s_foz)
    for k in range(1, 8):
        fo_z_in(k).wait_recv()
    fin_sib_in().wait_recv()
    left(FX.at[0:15], s_gx)
    left(FZ.at[0:15], s_gz)
    for k in range(1, 16):
        g_z_in(k).wait_recv()

    tiles = FZ[...].reshape(8, 2, 8, 128)
    grid = (tiles[:, 0] + tiles[:, 1]).reshape(64, 128)
    mean = jnp.sum(grid) / 256.0
    wide = jnp.broadcast_to(grid[:, None, :], (64, 16, 128)).reshape(1024, 128)
    rr = lax.broadcasted_iota(jnp.int32, (1024, 128), 0)
    cc = lax.broadcasted_iota(jnp.int32, (1024, 128), 1)
    mine = jnp.where(cc == lax.rem(rr, 16) // 4, wide, 0.0)
    centered = jnp.sum(mine, axis=1, keepdims=True) - mean
    scaled = (centered * FO3[...].reshape(1024, 128).astype(F32)).astype(BF16)
    delta = lax.dot_general(scaled, FIN[...].reshape(1024, kw), (((0,), (0,)), ((), ())),
                            preferred_element_type=F32)
    neww[...] = (WL[...].astype(F32) + step_scale / math.sqrt(1024.0) * delta[0:sr]).astype(BF16)


def local(tokens, target, weight, factor_out, factor_in):
    rows, kw = tokens.shape
    sr = weight.shape[0]
    half = 8 * sr
    width = factor_out.shape[2]
    any_spec = pl.BlockSpec(memory_space=pltpu.HBM)
    vm = pl.BlockSpec(memory_space=pltpu.VMEM)
    D = pltpu.SemaphoreType.DMA
    scratch = [
        pltpu.VMEM(factor_out.shape, BF16),
        pltpu.VMEM(factor_in.shape, BF16),
        pltpu.VMEM((4, rows, kw), BF16),
        pltpu.VMEM((4, 2, half + 16, kw), BF16),
        pltpu.VMEM((8, 4, 2, 16, kw), BF16),
        pltpu.VMEM((rows, kw), BF16),
        pltpu.VMEM((sr, kw), BF16),
        pltpu.VMEM((2, rows, half + 16), F32),
        pltpu.VMEM((16, width), F32),
        pltpu.VMEM((8, 8, 16, 128), BF16),
        pltpu.VMEM((8, 8, 16, 128), BF16),
        pltpu.VMEM((8, 8, 16, 128), BF16),
        pltpu.VMEM((16, kw), BF16),
        pltpu.VMEM((16, 8, 128), F32),
        pltpu.VMEM((16, 8, 128), F32),
        D((6,)), D((4,)), D((4,)), D((6,)), D((4,)), D((16,)), D((2, 16)), D((2, 8)), D((8,)),
        D((4,)), D((4,)), D((5,)), D((5,)), D(()), D((8,)), D((8,)), D((16,)), D((16,)),
        D((2, 4)), D((6,)), D(()), D((2, 16)), D((2,)), D((2,)), D((8,)), D(()), D(()), D((2, 5)), D(()),
        D(()), D(()), D(()), D(()),
    ]
    return pl.pallas_call(
        kernel,
        out_shape=(pltpu.VMEM((rows, kw), BF16), pltpu.VMEM((sr, kw), BF16)),
        in_specs=[any_spec] * 5,
        out_specs=(vm, vm),
        scratch_shapes=scratch,
        compiler_params=pltpu.CompilerParams(
            collective_id=0, has_side_effects=True, vmem_limit_bytes=56 * 1024 * 1024),
    )(tokens, target, weight, factor_out, factor_in)


def solution(mesh):
    from jax.sharding import PartitionSpec as P

    in_specs = (
        P("pop", "tp"),
        P("pop", "tp"),
        P("pop", "tp"),
        P("pop", None, None),
        P("pop", None, "tp"),
    )
    out_specs = (P("pop", "tp"), P("pop", "tp"))
    return jax.shard_map(local, mesh=mesh, in_specs=in_specs, out_specs=out_specs, check_vma=False)
```

time: 128 us -> 125 us (0.977)
  Pallas kernels: 125 us -> 122 us
    pallas_call x1, Pallas kernels: 125 us -> 122 us  [local(): pl.pallas_call(kernel, out_shape=(pltpu.VMEM((rows, kw), BF16), pltpu.VME...]
where the time goes in v3:
time: 125 us
  Pallas kernels  122 us (98%)
  local copies, waits for them, and re-layouts  2.17 us (2%)
    pallas_call x1, Pallas kernels, local(): pl.pallas_call(kernel, out_shape=(pltpu.VMEM((rows, kw), BF16), pltpu.VME...  122 us

profile of v3, /device:TPU:1, one launch (start us, length us, event | category | flops | bytes accessed | tf_op | source)
XLA Modules:
  0.0 124.6 jit_solution(16014695649466988913)
XLA Ops:
  0.6 121.8 %shard_map.68 = (bf16[1024,1280]{1,0:T(8,128)(2,1)S(1)}, bf16[80,1280]{1,0:T(8,128)(2,1)S(1)}) custom-call(bf16[1024,1280]{1,0:T(8,128)(2,1)} %tok.1, bf16[1024,1280]{1,0:T(8,128)(2,1)} %tgt.1, bf16[80,1280]{1,0:T(8,128)(2,1)} %wt.1, bf16[4,4,5120]{2,1,0:T(4,128)(2,1)} %fo_hbm.1, bf16[4,4,1280]{2,1,0:T(4,128)(2,1)} %fin_hbm.1), custom_call_target="tpu_custom_call" | custom-call | tf_op jit(solution)/shard_map/pallas_call | solution.py:548
  122.4 1.5 %copy.9 = bf16[1024,1280]{1,0:T(8,128)(2,1)} copy(bf16[1024,1280]{1,0:T(8,128)(2,1)S(1)} %get-tuple-element.2) | data formatting | bytes 5242880
  123.9 0.7 copy.10

commit v4 on v3

--- a/solution.py
+++ b/solution.py
@@ -100,16 +100,16 @@
 
     xslot = {1: 2, 2: 3, 3: 1}
     for k in range(1, 4):
-        rc(FP, W.at[xslot[k], 0, half:half + rank16], s_fx, fxs.at[k], p, lax.rem(x + k, 4)).start()
+        rc(FP, W.at[xslot[k], 0, half:half + rank16], s_fx, fxs, p, lax.rem(x + k, 4)).start()
 
     def chunk(m):
         return pl.ds(m * mem, mem)
 
     def tok_right(m):
-        return rc(tok.at[chunk(m)], T.at[2, chunk(m)], s_tok.at[0, m], tr.at[m], p, xr)
+        return rc(tok.at[chunk(m)], T.at[2, chunk(m)], s_tok, tr.at[m], p, xr)
 
     def tok_left(m):
-        return rc(tok.at[chunk(m)], T.at[1, chunk(m)], s_tok.at[1, m], tl.at[m], p, xl)
+        return rc(tok.at[chunk(m)], T.at[1, chunk(m)], s_tok, tl.at[m], p, xl)
 
     small = mem // 2
     pieces = ((0, 0, mem), (3, 3 * mem, mem), (1, mem, small), (2, 2 * mem + small, small),
@@ -119,28 +119,22 @@
         m, first, n = pieces[i]
         rws = pl.ds(first, n)
         side, to = (1, xl) if m >= 2 else (2, xr)
-        return rc(T.at[side, rws], T.at[3, rws], s_tf.at[i], tf.at[i], p, to)
+        return rc(T.at[side, rws], T.at[3, rws], s_tf, tf.at[i], p, to)
 
     for m in range(4):
         tok_right(m).start()
         tok_left(3 - m).start()
 
     def fin_y(k):
-        return rc(FP, FIN.at[z, y, c], s_fny, fny.at[k],
+        return rc(FP, FIN.at[z, y, c], s_fny, fny,
                   z * 8 + lax.rem(y + k, 4) * 2 + c, x)
-
-    def fin_y_in(k):
-        return rc(FP, FIN.at[z, lax.rem(y + 4 - k, 4), c], s_fny, fny.at[k], p, x)
 
     for k in range(1, 4):
         fin_y(k).start()
 
     def fo_y(k):
         ee = lax.rem(e + k, 8)
-        return rc(FOS.at[ee], FO2.at[e], s_foy, foy.at[k], z * 8 + ee, x)
-
-    def fo_y_in(k):
-        return rc(FOS.at[0], FO2.at[lax.rem(e + 8 - k, 8)], s_foy, foy.at[k], p, x)
+        return rc(FOS.at[ee], FO2.at[e], s_foy, foy, z * 8 + ee, x)
 
     def fo_cut():
         l_fo.wait()
@@ -163,10 +157,7 @@
 
     def fo_z(k):
         zz = lax.rem(z + k, 8)
-        return rc(FO2.at[:, zz], FO3.at[z], s_foz, foz.at[k], zz * 8 + e, x)
-
-    def fo_z_in(k):
-        return rc(FO2.at[:, 0], FO3.at[lax.rem(z + 8 - k, 8)], s_foz, foz.at[k], p, x)
+        return rc(FO2.at[:, zz], FO3.at[z], s_foz, foz, zz * 8 + e, x)
 
     l_wl.wait()
     l_t0.wait()
@@ -185,29 +176,26 @@
         return rc(shard_at(s, yy, h), shard_at(s, yy, h), ss, rs, pop, x)
 
     def z_send(s, h, d):
-        return piece(s, y, h, s_z.at[d, 2 * s + h], wz.at[2 * s + h], (zu, zd)[d])
+        return piece(s, y, h, s_z.at[d], wz.at[2 * s + h], (zu, zd)[d])
 
     def z_in(s, h):
-        return piece(s, y, h, s_z.at[0, 2 * s + h], wz.at[2 * s + h], p)
+        return piece(s, y, h, s_z.at[0], wz.at[2 * s + h], p)
 
     def y_send(s, h, d):
-        return piece(s, y, h, s_y.at[d], yin.at[d, 2 * s + h], (yup, ydn)[d])
-
-    def y_in(s, h, d):
-        return piece(s, y + (3, 1)[d], h, s_y.at[d], yin.at[d, 2 * s + h], p)
+        return piece(s, y, h, s_y.at[d], yin.at[2 * s + h], (yup, ydn)[d])
 
     def f_send(s, d):
-        return piece(s, y + (3, 1)[d], d, s_f.at[d], ff.at[d, s], (yup, ydn)[d])
-
-    def f_in(s, d):
-        return piece(s, y + 2, d, s_f.at[d], ff.at[d, s], p)
+        return piece(s, y + (3, 1)[d], d, s_f.at[d], ff.at[s], (yup, ydn)[d])
+
+    def arrived(ref, sem):
+        rc(ref, ref, s_wa, sem, p, x).wait_recv()
 
     def pass_on(s, k):
-        return rc(shard_at(s, y + k), shard_at(s, y + k), s_d2.at[s], d2.at[s], sib, x)
+        return rc(shard_at(s, y + k), shard_at(s, y + k), s_d2, d2.at[s], sib, x)
 
     def sib_in(s):
         whole = W.at[s // 2, s % 2, 0:4 * sr]
-        return rc(whole, whole, s_d2.at[s], d2.at[s], p, x)
+        return rc(whole, whole, s_d2, d2.at[s], p, x)
 
     def z_pred(s, d):
         if d == 0:
@@ -240,17 +228,14 @@
             pass_on(s, 0).start()
 
     def stage_b(s, h):
-        for d in range(2):
-            y_in(s, h, d).wait_recv()
-            if d == h:
-                f_send(s, d).start()
+        arrived(W.at[0, 0, 0:2 * sr, 0:kw // 2], yin.at[2 * s + h])
+        f_send(s, h).start()
         if h == 1:
             pass_on(s, 3).start()
             pass_on(s, 1).start()
 
     def stage_c(s):
-        for d in range(2):
-            f_in(s, d).wait_recv()
+        arrived(shard_at(s, y + 2), ff.at[s])
         pass_on(s, 2).start()
 
     def product(s, rws):
@@ -278,22 +263,22 @@
     def fin_up(h):
         lo, n = (0, 4) if h < 4 else (0, 2)
         ref = fin_block(z + 9 - h, lo, n)
-        return rc(ref, ref, s_fnz.at[0, h], fnu.at[h], zu, x)
+        return rc(ref, ref, s_fnz, fnu.at[h], zu, x)
 
     def fin_up_in(h):
         lo, n = (0, 4) if h < 4 else (0, 2)
         ref = fin_block(z + 8 - h, lo, n)
-        return rc(ref, ref, s_fnz.at[0, h], fnu.at[h], p, x)
+        return rc(ref, ref, s_fnz, fnu.at[h], p, x)
 
     def fin_dn(h):
         lo, n = (0, 4) if h < 4 else (2, 2)
         ref = fin_block(z + h - 1, lo, n)
-        return rc(ref, ref, s_fnz.at[1, h], fnd.at[h], zd, x)
+        return rc(ref, ref, s_fnz, fnd.at[h], zd, x)
 
     def fin_dn_in(h):
         lo, n = (0, 4) if h < 4 else (2, 2)
         ref = fin_block(z + h, lo, n)
-        return rc(ref, ref, s_fnz.at[1, h], fnd.at[h], p, x)
+        return rc(ref, ref, s_fnz, fnd.at[h], p, x)
 
     def fin_sib():
         ref = FIN.at[:, :, c]
@@ -339,8 +324,7 @@
 
     def fin_hop(h):
         if h == 1:
-            for k in range(1, 4):
-                fin_y_in(k).wait_recv()
+            arrived(FIN.at[z, 0:3, c], fny)
         else:
             fin_up_in(h - 1).wait_recv()
             fin_dn_in(h - 1).wait_recv()
@@ -348,14 +332,12 @@
         fin_dn(h).start()
 
     def tokens_in():
-        for k in range(1, 4):
-            rc(FP, W.at[xslot[k], 0, half:half + rank16], s_fx, fxs.at[k], p, x).wait_recv()
+        arrived(W.at[0, 0, 0:3 * rank16], fxs)
         for m in (0, 1):
             tok_left(m).wait_recv()
 
     def fo_hop():
-        for k in range(1, 8):
-            fo_y_in(k).wait_recv()
+        arrived(FO2.at[0:7], foy)
         for k in range(1, 8):
             fo_z(k).start()
         FO3[z] = FO2[:, z]
@@ -443,12 +425,11 @@
 
     def g_x(k):
         pop, tp = xy_peer(k)
-        return rc(FX.at[0], FX.at[k], s_gx, gx.at[k], pop, tp)
+        return rc(FX.at[0], FX.at[k], s_gx, gx, pop, tp)
 
     for k in range(1, 16):
         g_x(k).start()
-    for k in range(1, 16):
-        g_x(k).wait_recv()
+    arrived(FX.at[1:16], gx)
     plane = FX[0]
     for k in range(1, 16):
         plane = plane + FX[k]
@@ -456,11 +437,7 @@
 
     def g_z(k):
         ref = FZ.at[z * 2 + c]
-        return rc(ref, ref, s_gz, gz.at[k], zc_peer(k), x)
-
-    def g_z_in(k):
-        ref = FZ.at[lax.rem(z + 8 - k % 8, 8) * 2 + lax.rem(c + k // 8, 2)]
-        return rc(ref, ref, s_gz, gz.at[k], p, x)
+        return rc(ref, ref, s_gz, gz, zc_peer(k), x)
 
     for k in range(1, 16):
         g_z(k).start()
@@ -473,34 +450,38 @@
 
     left(FIN.at[0, 0:3, 0], s_fx)
     left(FIN.at[0, 0:3, 0], s_fny)
-    for m in range(4):
-        tok_right(m).wait_send()
-        tok_left(m).wait_send()
-    for i in range(6):
-        tok_fwd(i).wait_send()
-    for s in range(NSTEP):
-        for d in range(2):
-            for h in range(2):
-                @pl.when(z_pred(s, d))
-                def _():
-                    z_send(s, h, d).wait_send()
-        left(W.at[0, 0, 0:4 * sr], s_d2.at[s])
+    left(T.at[0:2], s_tok)
+    left(T.at[0], s_tf)
+
+    @pl.when((rz >= 1) & (rz <= 3))
+    def _():
+        left(W.at[0, 0, 0:8 * sr], s_z.at[0])
+
+    @pl.when(rz == 0)
+    def _():
+        left(W.at[0, 0, 0:4 * sr], s_z.at[0])
+
+    @pl.when((rz == 0) | (rz >= 6))
+    def _():
+        left(W.at[0, 0, 0:8 * sr], s_z.at[1])
+
+    @pl.when(rz == 1)
+    def _():
+        left(W.at[0, 0, 0:4 * sr], s_z.at[1])
+
     for d in range(2):
         left(W.at[0, 0, 0:8 * sr], s_y.at[d])
         left(W.at[0, 0, 0:4 * sr], s_f.at[d])
-    for h in range(1, 5):
-        fin_up(h).wait_send()
-        fin_dn(h).wait_send()
+    left(W.at[0:2, :, 0:8 * sr], s_d2)
+    left(FIN.at[0:7, :, 0], s_fnz)
     fin_sib().wait_send()
     left(FOS.at[0:7], s_foy)
     left(FO3.at[0:7], s_foz)
-    for k in range(1, 8):
-        fo_z_in(k).wait_recv()
+    arrived(FO3.at[0:7], foz)
     fin_sib_in().wait_recv()
     left(FX.at[0:15], s_gx)
     left(FZ.at[0:15], s_gz)
-    for k in range(1, 16):
-        g_z_in(k).wait_recv()
+    arrived(FZ.at[0:15], gz)
 
     tiles = FZ[...].reshape(8, 2, 8, 128)
     grid = (tiles[:, 0] + tiles[:, 1]).reshape(64, 128)
@@ -540,9 +521,9 @@
         pltpu.VMEM((16, kw), BF16),
         pltpu.VMEM((16, 8, 128), F32),
         pltpu.VMEM((16, 8, 128), F32),
-        D((6,)), D((4,)), D((4,)), D((6,)), D((4,)), D((16,)), D((2, 16)), D((2, 8)), D((8,)),
-        D((4,)), D((4,)), D((5,)), D((5,)), D(()), D((8,)), D((8,)), D((16,)), D((16,)),
-        D((2, 4)), D((6,)), D(()), D((2, 16)), D((2,)), D((2,)), D((8,)), D(()), D(()), D((2, 5)), D(()),
+        D((6,)), D((4,)), D((4,)), D((6,)), D((4,)), D((16,)), D((16,)), D((8,)), D((8,)),
+        D(()), D(()), D((5,)), D((5,)), D(()), D(()), D(()), D(()), D(()),
+        D(()), D(()), D(()), D((2,)), D((2,)), D((2,)), D(()), D(()), D(()), D(()), D(()),
         D(()), D(()), D(()), D(()),
     ]
     return pl.pallas_call(

time: 125 us -> 124 us (level)
  no operation moved by 1% of the time
where the time goes in v4:
time: 124 us; the launch traced here: 123 us
  Pallas kernels  121 us (98%)
  local copies, waits for them, and re-layouts  2.17 us (2%)
    pallas_call x1, Pallas kernels, local(): pl.pallas_call(kernel, out_shape=(pltpu.VMEM((rows, kw), BF16), pltpu.VME...  121 us

profile of v4, /device:TPU:1, one launch (start us, length us, event | category | flops | bytes accessed | tf_op | source)
XLA Modules:
  0.0 123.4 jit_solution(3434679546244839000)
XLA Ops:
  0.6 120.6 %shard_map.68 = (bf16[1024,1280]{1,0:T(8,128)(2,1)S(1)}, bf16[80,1280]{1,0:T(8,128)(2,1)S(1)}) custom-call(bf16[1024,1280]{1,0:T(8,128)(2,1)} %tok.1, bf16[1024,1280]{1,0:T(8,128)(2,1)} %tgt.1, bf16[80,1280]{1,0:T(8,128)(2,1)} %wt.1, bf16[4,4,5120]{2,1,0:T(4,128)(2,1)} %fo_hbm.1, bf16[4,4,1280]{2,1,0:T(4,128)(2,1)} %fin_hbm.1), custom_call_target="tpu_custom_call" | custom-call | tf_op jit(solution)/shard_map/pallas_call | solution.py:529
  121.2 1.5 %copy.9 = bf16[1024,1280]{1,0:T(8,128)(2,1)} copy(bf16[1024,1280]{1,0:T(8,128)(2,1)S(1)} %get-tuple-element.2) | data formatting | bytes 5242880
  122.7 0.7 copy.10

commit v5 on v4

--- a/solution.py
+++ b/solution.py
@@ -16,9 +16,9 @@
 
 
 def kernel(tok, tgt, wt, fo_hbm, fin_hbm, out, neww,
-           fo, fin, T, W, FIN, TG, WL, ACC, S32, FOS, FO2, FO3, FP, FX, FZ,
+           fo, fin, T, W, FIN, TG, WL, ACC, S32, FOS, FO2, FO3, FP, FX, FZ, STG,
            loc, tr, tl, tf, wa, wz, yin, ff, d2, fxs, fny, fnu, fnd, fnc,
-           foy, foz, gx, gz,
+           foy, foz, gx, gz, st, s_rl,
            s_tok, s_tf, s_wa, s_z, s_y, s_f, s_d2, s_fx, s_fny, s_fnz, s_fnc, s_foy, s_foz, s_gx, s_gz):
     p = lax.axis_index("pop")
     x = lax.axis_index("tp")
@@ -73,6 +73,68 @@
     for pop, tp in partners:
         pl.semaphore_signal(bar, inc=1, device_id={"pop": pop, "tp": tp},
                             device_id_type=pl.DeviceIdType.MESH)
+    pl.semaphore_wait(bar, 33)
+
+    zt = z // 2
+    r_own = lax.rem(z, 2)
+    off = lax.rem(x - zt + 4, 4)
+    slot = off + off // 2 - 2 * (off // 3)
+    shard = pl.ds(pl.multiple_of(e * sr, 16), sr)
+    send_a = rc(wt, W.at[slot, r_own, shard], s_wa, wa.at[slot], p, zt)
+    copy_a = pltpu.make_async_copy(wt, W.at[0, r_own, shard], loc.at[3])
+
+    @pl.when(off == 0)
+    def _():
+        copy_a.start()
+
+    def half_of(h):
+        return pl.ds(h * (kw // 2), kw // 2)
+
+    def split_a(h):
+        return rc(wt.at[:, half_of(h)], STG, s_wa, st, p, (xl, xr)[h])
+
+    def relay(h):
+        return rc(STG, W.at[3, r_own, shard, half_of(h)], s_rl, wa.at[3], p, (xl, xr)[h])
+
+    @pl.when((off == 1) | (off == 3))
+    def _():
+        send_a.start()
+
+    @pl.when(off == 2)
+    def _():
+        split_a(0).start()
+        split_a(1).start()
+
+    xslot = {1: 2, 2: 3, 3: 1}
+    def chunk(m):
+        return pl.ds(m * mem, mem)
+
+    def tok_right(m):
+        return rc(tok.at[chunk(m)], T.at[2, chunk(m)], s_tok, tr.at[m], p, xr)
+
+    def tok_left(m):
+        return rc(tok.at[chunk(m)], T.at[1, chunk(m)], s_tok, tl.at[m], p, xl)
+
+    small = mem // 2
+    pieces = ((0, 0, mem), (3, 3 * mem, mem), (1, mem, small), (2, 2 * mem + small, small),
+              (1, mem + small, small), (2, 2 * mem, small))
+
+    def tok_fwd(i):
+        m, first, n = pieces[i]
+        rws = pl.ds(first, n)
+        side, to = (1, xl) if m >= 2 else (2, xr)
+        return rc(T.at[side, rws], T.at[3, rws], s_tf, tf.at[i], p, to)
+
+    for m in range(4):
+        tok_right(m).start()
+        tok_left(3 - m).start()
+        if m == 0:
+            for h in range(2):
+                @pl.when(off == 1 + 2 * h)
+                def _():
+                    rc(STG, STG, s_rl, st, p, x).wait_recv()
+                    relay(h).start()
+
     l_fi.wait()
     for i in range(4):
         S32[4 * i:4 * i + 4, 0:kw] = fin[i].astype(F32)
@@ -80,57 +142,10 @@
     FP[...] = fin16
     FIN[z, y, c] = fin16
     W[0, 0, half:half + rank16] = fin16
-    pl.semaphore_wait(bar, 33)
-
-    zt = z // 2
-    r_own = lax.rem(z, 2)
-    off = lax.rem(x - zt + 4, 4)
-    slot = off + off // 2 - 2 * (off // 3)
-    shard = pl.ds(pl.multiple_of(e * sr, 16), sr)
-    send_a = rc(wt, W.at[slot, r_own, shard], s_wa, wa.at[slot], p, zt)
-    copy_a = pltpu.make_async_copy(wt, W.at[0, r_own, shard], loc.at[3])
-
-    @pl.when(off == 0)
-    def _():
-        copy_a.start()
-
-    @pl.when(off != 0)
-    def _():
-        send_a.start()
-
-    xslot = {1: 2, 2: 3, 3: 1}
-    for k in range(1, 4):
-        rc(FP, W.at[xslot[k], 0, half:half + rank16], s_fx, fxs, p, lax.rem(x + k, 4)).start()
-
-    def chunk(m):
-        return pl.ds(m * mem, mem)
-
-    def tok_right(m):
-        return rc(tok.at[chunk(m)], T.at[2, chunk(m)], s_tok, tr.at[m], p, xr)
-
-    def tok_left(m):
-        return rc(tok.at[chunk(m)], T.at[1, chunk(m)], s_tok, tl.at[m], p, xl)
-
-    small = mem // 2
-    pieces = ((0, 0, mem), (3, 3 * mem, mem), (1, mem, small), (2, 2 * mem + small, small),
-              (1, mem + small, small), (2, 2 * mem, small))
-
-    def tok_fwd(i):
-        m, first, n = pieces[i]
-        rws = pl.ds(first, n)
-        side, to = (1, xl) if m >= 2 else (2, xr)
-        return rc(T.at[side, rws], T.at[3, rws], s_tf, tf.at[i], p, to)
-
-    for m in range(4):
-        tok_right(m).start()
-        tok_left(3 - m).start()
-
     def fin_y(k):
         return rc(FP, FIN.at[z, y, c], s_fny, fny,
                   z * 8 + lax.rem(y + k, 4) * 2 + c, x)
 
-    for k in range(1, 4):
-        fin_y(k).start()
 
     def fo_y(k):
         ee = lax.rem(e + k, 8)
@@ -345,6 +360,10 @@
     A, B, C = stage_a, stage_b, stage_c
     A(0, 0)
     A(0, 1)
+    for k in range(1, 4):
+        rc(FP, W.at[xslot[k], 0, half:half + rank16], s_fx, fxs, p, lax.rem(x + k, 4)).start()
+    for k in range(1, 4):
+        fin_y(k).start()
     fo_cut()
     A(1, 0)
     B(0, 0)
@@ -448,6 +467,11 @@
     def _():
         send_a.wait_send()
 
+    for h in range(2):
+        @pl.when(off == 1 + 2 * h)
+        def _():
+            relay(h).wait_send()
+
     left(FIN.at[0, 0:3, 0], s_fx)
     left(FIN.at[0, 0:3, 0], s_fny)
     left(T.at[0:2], s_tok)
@@ -521,8 +545,9 @@
         pltpu.VMEM((16, kw), BF16),
         pltpu.VMEM((16, 8, 128), F32),
         pltpu.VMEM((16, 8, 128), F32),
+        pltpu.VMEM((sr, kw // 2), BF16),
         D((6,)), D((4,)), D((4,)), D((6,)), D((4,)), D((16,)), D((16,)), D((8,)), D((8,)),
-        D(()), D(()), D((5,)), D((5,)), D(()), D(()), D(()), D(()), D(()),
+        D(()), D(()), D((5,)), D((5,)), D(()), D(()), D(()), D(()), D(()), D(()), D(()),
         D(()), D(()), D(()), D((2,)), D((2,)), D((2,)), D(()), D(()), D(()), D(()), D(()),
         D(()), D(()), D(()), D(()),
     ]

time: 124 us -> 122 us (0.984)
  Pallas kernels: 121 us -> 119 us
    pallas_call x1, Pallas kernels: 121 us -> 119 us  [local(): pl.pallas_call(kernel, out_shape=(pltpu.VMEM((rows, kw), BF16), pltpu.VME...]
where the time goes in v5:
time: 122 us
  Pallas kernels  119 us (98%)
  local copies, waits for them, and re-layouts  2.17 us (2%)
    pallas_call x1, Pallas kernels, local(): pl.pallas_call(kernel, out_shape=(pltpu.VMEM((rows, kw), BF16), pltpu.VME...  119 us

profile of v5, /device:TPU:1, one launch (start us, length us, event | category | flops | bytes accessed | tf_op | source)
XLA Modules:
  0.0 121.7 jit_solution(8977174426999063571)
XLA Ops:
  0.6 118.9 %shard_map.68 = (bf16[1024,1280]{1,0:T(8,128)(2,1)S(1)}, bf16[80,1280]{1,0:T(8,128)(2,1)S(1)}) custom-call(bf16[1024,1280]{1,0:T(8,128)(2,1)} %tok.1, bf16[1024,1280]{1,0:T(8,128)(2,1)} %tgt.1, bf16[80,1280]{1,0:T(8,128)(2,1)} %wt.1, bf16[4,4,5120]{2,1,0:T(4,128)(2,1)} %fo_hbm.1, bf16[4,4,1280]{2,1,0:T(4,128)(2,1)} %fin_hbm.1), custom_call_target="tpu_custom_call" | custom-call | tf_op jit(solution)/shard_map/pallas_call | solution.py:554
  119.5 1.5 %copy.9 = bf16[1024,1280]{1,0:T(8,128)(2,1)} copy(bf16[1024,1280]{1,0:T(8,128)(2,1)S(1)} %get-tuple-element.2) | data formatting | bytes 5242880
  121.0 0.7 copy.10

commit v6 on v5

--- a/solution.py
+++ b/solution.py
@@ -16,7 +16,7 @@
 
 
 def kernel(tok, tgt, wt, fo_hbm, fin_hbm, out, neww,
-           fo, fin, T, W, FIN, TG, WL, ACC, S32, FOS, FO2, FO3, FP, FX, FZ, STG,
+           fo, fin, T, W, FIN, TG, WL, ACC, S32, FOS, FO2, FO3, FP, FX, FZ, STG, FIT,
            loc, tr, tl, tf, wa, wz, yin, ff, d2, fxs, fny, fnu, fnd, fnc,
            foy, foz, gx, gz, st, s_rl,
            s_tok, s_tf, s_wa, s_z, s_y, s_f, s_d2, s_fx, s_fny, s_fnz, s_fnc, s_foy, s_foz, s_gx, s_gz):
@@ -115,9 +115,9 @@
     def tok_left(m):
         return rc(tok.at[chunk(m)], T.at[1, chunk(m)], s_tok, tl.at[m], p, xl)
 
-    small = mem // 2
-    pieces = ((0, 0, mem), (3, 3 * mem, mem), (1, mem, small), (2, 2 * mem + small, small),
-              (1, mem + small, small), (2, 2 * mem, small))
+    small = mem // 4
+    pieces = ((0, 0, mem), (3, 3 * mem, mem), (1, mem, mem - small), (2, 2 * mem + small, mem - small),
+              (1, 2 * mem - small, small), (2, 2 * mem, small))
 
     def tok_fwd(i):
         m, first, n = pieces[i]
@@ -322,10 +322,11 @@
                 lo, outer, preferred_element_type=F32)
             full = ACC[r, rws, 0:half] * base_factor + low * low_factor
             out[rws, cols] = full.astype(BF16)
-            part = jnp.sum(full * TG[rws, cols].astype(F32)) / (mem * math.sqrt(width_out))
-            FX[0] += jnp.where((sub == e) & (lanes == m), part, 0.0)
-
-    FX[0] = jnp.zeros((8, 128), F32)
+            part = jnp.sum((full * TG[rws, cols].astype(F32)).reshape(n // 8, 8, half), axis=0)
+            for i in range(half // 128):
+                FIT[m] += part[:, i * 128:(i + 1) * 128]
+
+    FIT[...] = jnp.zeros(FIT.shape, F32)
 
     zone = (rz <= 1, (rz == 2) | (rz == 7), (rz >= 3) & (rz <= 6))
 
@@ -430,7 +431,7 @@
             tok_fwd(i).wait_recv()
         if pair[0] == 4:
             for k in (6, 7):
-                product(k, pl.ds(mem + small, mem))
+                product(k, pl.ds(2 * mem - small, 2 * small))
         for i in pair:
             m, first, n = pieces[i]
             if pair[0] < 4:
@@ -446,6 +447,11 @@
         pop, tp = xy_peer(k)
         return rc(FX.at[0], FX.at[k], s_gx, gx, pop, tp)
 
+    tile = jnp.zeros((8, 128), F32)
+    for m in range(4):
+        total = jnp.sum(FIT[m]) / (mem * math.sqrt(width_out))
+        tile = tile + jnp.where((sub == e) & (lanes == m), total, 0.0)
+    FX[0] = tile
     for k in range(1, 16):
         g_x(k).start()
     arrived(FX.at[1:16], gx)
@@ -546,6 +552,7 @@
         pltpu.VMEM((16, 8, 128), F32),
         pltpu.VMEM((16, 8, 128), F32),
         pltpu.VMEM((sr, kw // 2), BF16),
+        pltpu.VMEM((4, 8, 128), F32),
         D((6,)), D((4,)), D((4,)), D((6,)), D((4,)), D((16,)), D((16,)), D((8,)), D((8,)),
         D(()), D(()), D((5,)), D((5,)), D(()), D(()), D(()), D(()), D(()), D(()), D(()),
         D(()), D(()), D(()), D((2,)), D((2,)), D((2,)), D(()), D(()), D(()), D(()), D(()),

time: 122 us -> 121 us (level)
  no operation moved by 1% of the time
where the time goes in v6:
time: 121 us
  Pallas kernels  119 us (98%)
  local copies, waits for them, and re-layouts  2.17 us (2%)
    pallas_call x1, Pallas kernels, local(): pl.pallas_call(kernel, out_shape=(pltpu.VMEM((rows, kw), BF16), pltpu.VME...  119 us

profile of v6, /device:TPU:1, one launch (start us, length us, event | category | flops | bytes accessed | tf_op | source)
XLA Modules:
  0.0 121.4 jit_solution(3796074796053766116)
XLA Ops:
  0.6 118.5 %shard_map.68 = (bf16[1024,1280]{1,0:T(8,128)(2,1)S(1)}, bf16[80,1280]{1,0:T(8,128)(2,1)S(1)}) custom-call(bf16[1024,1280]{1,0:T(8,128)(2,1)} %tok.1, bf16[1024,1280]{1,0:T(8,128)(2,1)} %tgt.1, bf16[80,1280]{1,0:T(8,128)(2,1)} %wt.1, bf16[4,4,5120]{2,1,0:T(4,128)(2,1)} %fo_hbm.1, bf16[4,4,1280]{2,1,0:T(4,128)(2,1)} %fin_hbm.1), custom_call_target="tpu_custom_call" | custom-call | tf_op jit(solution)/shard_map/pallas_call | solution.py:561
  119.2 1.5 %copy.9 = bf16[1024,1280]{1,0:T(8,128)(2,1)} copy(bf16[1024,1280]{1,0:T(8,128)(2,1)S(1)} %get-tuple-element.2) | data formatting | bytes 5242880
  120.7 0.7 copy.10
